TPU v7x, 32 devices: a whole 2x2x4 slice. The times are simulated.
32 devices in a mesh: shard: 8 (over y, x, core), model: 4 (over z).
Axes of the slice: x: 2, y: 2, z: 4, core: 2. Of those that a mesh axis runs over, the one named last changes fastest.
Arguments:
- weight_gate: float32 [3072, 8192], P('shard', 'model'), may hold values from -0.15625 to 0.15625
- smooth_gate: float32 [3072, 8192], P('shard', 'model'), may hold values from -0.109375 to 0.109375
- weight_up: float32 [3072, 8192], P('shard', 'model'), may hold values from -0.15625 to 0.15625
- smooth_up: float32 [3072, 8192], P('shard', 'model'), may hold values from -0.109375 to 0.109375
- norm_train: float32 [3072], P(('shard', 'model')), may hold values from 0.25 to 1.75
- norm_step: float32 [3072], P(('shard', 'model')), may hold values from -0.3 to 0.3
Outputs:
- serving_gate: bfloat16 [3072, 8192], P(None, 'model')
- serving_up: bfloat16 [3072, 8192], P(None, 'model')
- factor_gate: float32 [8192], P('model')
- factor_up: float32 [8192], P('model')
- serve_norm: bfloat16 [3072], replicated
- whole_gate: float32 [3072, 8192], P('shard', 'model')
- whole_up: float32 [3072, 8192], P('shard', 'model')
All inputs are finite; a program needn't handle non-finite values. Where the computation divides by a largest or mean magnitude, that divisor is 1e-20 or more.
Results may differ from a plain program's by a relative error of at most 0.001.
Values may be sent and summed in bfloat16 or wider, within the bound.
A program may use at most 128 MiB of HBM per device.

v0:
```python
import functools
import math

import jax
import jax.numpy as jnp
from jax import lax
from jax.experimental import pallas as pl
from jax.experimental.pallas import tpu as pltpu
from jax.sharding import PartitionSpec as P

MESH = pl.DeviceIdType.MESH
keep_rate = 0.7


def grid_of(n_shard):
    chips = n_shard // 2
    nx = math.isqrt(chips)
    while chips % nx:
        nx -= 1
    return chips // nx, nx


def kernel(
    n_shard, n_model, ny, nx, pieces,
    weight_gate, smooth_gate, weight_up, smooth_up, norm_train, norm_step,
    serve_gate, serve_up, factor_gate, factor_up, norm_all, whole_gate, whole_up,
    weights, smooths, peaks, norm_in,
    load_sem, norm_load, peak_send, peak_recv, norm_send, norm_recv, row_send, row_recv,
    x_send, y_send, pair_send, ring_recv, pair_recv,
):
    me = lax.axis_index("shard")
    col = lax.axis_index("model")
    core = lax.rem(me, 2)
    chip = me // 2
    xpos, ypos = lax.rem(chip, nx), chip // nx
    x_next = (ypos * nx + lax.rem(xpos + 1, nx)) * 2 + core
    y_next = (lax.rem(ypos + 1, ny) * nx + xpos) * 2 + core
    pair = chip * 2 + (1 - core)
    rows, cols = whole_gate.shape
    part = cols // pieces
    serves, wholes, factors = (serve_gate, serve_up), (whole_gate, whole_up), (factor_gate, factor_up)

    norm_loads = [
        pltpu.make_async_copy(src, norm_in.at[i], norm_load.at[i]) for i, src in enumerate((norm_train, norm_step))
    ]
    for copy in norm_loads:
        copy.start()
    loads = {}
    for unit, (w_ref, s_ref) in enumerate(((weight_gate, smooth_gate), (weight_up, smooth_up))):
        for k in sorted(range(pieces), key=lambda k: k % max(1, pieces // 2)):
            span = pl.ds(k * part, part)
            for which, (src, dst) in enumerate(((w_ref, weights), (s_ref, smooths))):
                copy = pltpu.make_async_copy(src.at[:, span], dst.at[unit, :, span], load_sem.at[unit, k, which])
                copy.start()
                loads[unit, k, which] = copy

    barrier = pltpu.get_barrier_semaphore()
    for d in range(1, n_shard):
        pl.semaphore_signal(barrier, inc=1, device_id=(lax.rem(me + d, n_shard), col), device_id_type=MESH)
    for d in range(1, n_model):
        pl.semaphore_signal(barrier, inc=1, device_id=(me, lax.rem(col + d, n_model)), device_id_type=MESH)

    per = norm_train.shape[1]
    for copy in norm_loads:
        copy.wait()
    norm_all[me, col, :, 0:per] = norm_in[0] + norm_in[1]

    def average(unit, k):
        for which in range(2):
            loads[unit, k, which].wait()
        across = pl.ds(k * part, part)

        def step(i, top):
            span = pl.ds(pl.multiple_of(i * 8, 8), 8)
            value = keep_rate * smooths[unit, span, across] + (1.0 - keep_rate) * weights[unit, span, across]
            wholes[unit][span, across] = value
            return jnp.maximum(top, jnp.abs(value))

        top = lax.fori_loop(0, rows // 8, step, jnp.zeros((8, part), jnp.float32), unroll=4)
        peaks[unit, k, me] = jnp.max(top, axis=0, keepdims=True)

    def send_peaks(unit, k):
        copies = []
        for d in range(1, n_shard):
            copy = pltpu.make_async_remote_copy(
                src_ref=peaks.at[unit, k, me], dst_ref=peaks.at[unit, k, me],
                send_sem=peak_send.at[unit, k, d - 1], recv_sem=peak_recv.at[unit, k, d - 1],
                device_id=(lax.rem(me + d, n_shard), col), device_id_type=MESH,
            )
            copy.start()
            copies.append(copy)
        return copies

    order = [(unit, k) for unit in range(2) for k in sorted(range(pieces), key=lambda k: k % max(1, pieces // 2))]
    peak_copies = {}
    norm_copies = []
    for n, (unit, k) in enumerate(order):
        average(unit, k)
        if n == 0:
            pl.semaphore_wait(barrier, n_shard + n_model - 2)
        peak_copies[unit, k] = send_peaks(unit, k)
    for d in range(1, n_model):
        copy = pltpu.make_async_remote_copy(
            src_ref=norm_all.at[me, col], dst_ref=norm_all.at[me, col],
            send_sem=norm_send.at[d - 1], recv_sem=norm_recv.at[d - 1],
            device_id=(me, lax.rem(col + d, n_model)), device_id_type=MESH,
        )
        copy.start()
        norm_copies.append(copy)

    def piece_of(unit, dy, dx, k, side):
        owner = (lax.rem(ypos - dy + ny, ny) * nx + lax.rem(xpos - dx + nx, nx)) * 2 + side
        return serves[unit].at[k, pl.ds(pl.multiple_of(owner * rows, rows), rows)]

    sent = []

    def start(unit, dy, dx, k, device, send_sem, recv_sem):
        ref = piece_of(unit, dy, dx, k, core)
        copy = pltpu.make_async_remote_copy(
            src_ref=ref, dst_ref=ref, send_sem=send_sem, recv_sem=recv_sem,
            device_id=(device, col), device_id_type=MESH,
        )
        copy.start()
        sent.append(copy)

    def along_x_first(unit, k):
        return 2 * k < pieces if pieces > 1 else unit == 0

    def to_x(unit, dy, dx, k):
        if dx < nx - 1 and (dy == 0 or not along_x_first(unit, k)):
            start(unit, dy, dx, k, x_next, x_send.at[unit, dy, dx, k], ring_recv.at[unit, dy, dx + 1, k])

    def to_y(unit, dy, dx, k):
        if dy < ny - 1 and (dx == 0 or along_x_first(unit, k)):
            start(unit, dy, dx, k, y_next, y_send.at[unit, dy, dx, k], ring_recv.at[unit, dy + 1, dx, k])

    def to_pair(unit, dy, dx, k):
        start(unit, dy, dx, k, pair, pair_send.at[unit, dy, dx, k], pair_recv.at[unit, dy, dx, k])

    def arrived(unit, dy, dx, k):
        ref = piece_of(unit, dy, dx, k, core)
        pltpu.make_async_copy(ref, ref, ring_recv.at[unit, dy, dx, k]).wait()

    def first_way(unit, k):
        (to_x if along_x_first(unit, k) else to_y)(unit, 0, 0, k)

    before = None
    for unit, k in order:
        across = pl.ds(k * part, part)
        for copy in peak_copies[unit, k]:
            copy.wait_recv()
        factor = peaks[unit, k, 0]
        for d in range(1, n_shard):
            factor = jnp.maximum(factor, peaks[unit, k, d])
        factors[unit][:, across] = factor
        if before:
            first_way(*before)

        def narrow(i, carry):
            at = i * 16
            value = wholes[unit][pl.ds(pl.multiple_of(at, 16), 16), across] / factors[unit][:, across]
            serves[unit][k, pl.ds(pl.multiple_of(me * rows + at, 16), 16)] = value.astype(jnp.bfloat16)
            return carry

        lax.fori_loop(0, rows // 16, narrow, 0, unroll=2)
        before = (unit, k)
    for copy in norm_copies:
        copy.wait_recv()
    row_copies = []
    for d in range(1, n_shard):
        copy = pltpu.make_async_remote_copy(
            src_ref=norm_all.at[me], dst_ref=norm_all.at[me],
            send_sem=row_send.at[d - 1], recv_sem=row_recv.at[d - 1],
            device_id=(lax.rem(me + d, n_shard), col), device_id_type=MESH,
        )
        copy.start()
        row_copies.append(copy)
    first_way(*before)
    for unit, k in order:
        (to_y if along_x_first(unit, k) else to_x)(unit, 0, 0, k)
    for unit, k in order:
        to_pair(unit, 0, 0, k)

    for distance in range(1, ny + nx - 1):
        for own_way in (True, False):
            for unit, k in order:
                for dy in range(ny):
                    dx = distance - dy
                    straight = (dy if along_x_first(unit, k) else dx) == 0
                    if 0 <= dx < nx and straight == own_way:
                        arrived(unit, dy, dx, k)
                        to_x(unit, dy, dx, k)
                        to_y(unit, dy, dx, k)
                        to_pair(unit, dy, dx, k)

    for unit in range(2):
        for dy in range(ny):
            for dx in range(nx):
                for k in range(pieces):
                    ref = piece_of(unit, dy, dx, k, 1 - core)
                    pltpu.make_async_copy(ref, ref, pair_recv.at[unit, dy, dx, k]).wait()
    for copy in sent + sum(peak_copies.values(), []) + norm_copies + row_copies:
        copy.wait_send()
    for copy in row_copies:
        copy.wait_recv()


def store_kernel(count, *refs):
    copies = []

    def move(src, dst):
        copies.append(pltpu.make_async_copy(src, dst, refs[-1].at[len(copies)]))
        copies[-1].start()

    for src, dst in zip(refs[:count], refs[count:-1]):
        if src.shape == dst.shape:
            move(src, dst)
            continue
        pieces, rows, part = src.shape
        for k in range(pieces):
            for half in range(2):
                span = pl.ds(half * (rows // 2), rows // 2)
                move(src.at[k, span], dst.at[span, pl.ds(k * part, part)])
    for copy in copies:
        copy.wait()


def store(arrays, shapes):
    hbm = pl.BlockSpec(memory_space=pltpu.HBM)
    return pl.pallas_call(
        functools.partial(store_kernel, len(arrays)),
        out_shape=tuple(pltpu.HBM(shape, a.dtype) for a, shape in zip(arrays, shapes)),
        in_specs=[pl.BlockSpec(memory_space=pltpu.VMEM)] * len(arrays),
        out_specs=(hbm,) * len(arrays),
        scratch_shapes=[pltpu.SemaphoreType.DMA((len(arrays) + 4 * arrays[0].shape[0],))],
        compiler_params=pltpu.CompilerParams(vmem_limit_bytes=1024 * 1024),
    )(*(pltpu.with_memory_space_constraint(a, pltpu.VMEM) for a in arrays))


def solution(mesh):
    n_shard, n_model = mesh.shape["shard"], mesh.shape["model"]
    ny, nx = grid_of(n_shard)

    def body(weight_gate, smooth_gate, weight_up, smooth_up, norm_train, norm_step):
        rows, cols = weight_gate.shape
        per = norm_train.shape[0]
        pieces = math.gcd(max(1, 16 // (ny * nx)), cols // 128)
        wide = -(-per // 128) * 128
        vmem = pl.BlockSpec(memory_space=pltpu.VMEM)
        hbm = pl.BlockSpec(memory_space=pltpu.HBM)
        dma = pltpu.SemaphoreType.DMA
        full = (pieces, n_shard * rows, cols // pieces)
        landed = pl.pallas_call(
            functools.partial(kernel, n_shard, n_model, ny, nx, pieces),
            out_shape=(
                pltpu.VMEM(full, jnp.bfloat16),
                pltpu.VMEM(full, jnp.bfloat16),
                pltpu.VMEM((1, cols), jnp.float32),
                pltpu.VMEM((1, cols), jnp.float32),
                pltpu.VMEM((n_shard, n_model, 1, wide), jnp.float32),
                pltpu.VMEM((rows, cols), jnp.float32),
                pltpu.VMEM((rows, cols), jnp.float32),
            ),
            in_specs=[hbm] * 6,
            out_specs=(vmem,) * 7,
            scratch_shapes=[
                pltpu.VMEM((2, rows, cols), jnp.float32),
                pltpu.VMEM((2, rows, cols), jnp.float32),
                pltpu.VMEM((2, pieces, n_shard, 1, cols // pieces), jnp.float32),
                pltpu.VMEM((2, 1, per), jnp.float32),
                dma((2, pieces, 2)),
                dma((2,)),
                dma((2, pieces, n_shard)),
                dma((2, pieces, n_shard)),
                dma((n_model,)),
                dma((n_model,)),
                dma((n_shard,)),
                dma((n_shard,)),
                dma((2, ny, nx, pieces)),
                dma((2, ny, nx, pieces)),
                dma((2, ny, nx, pieces)),
                dma((2, ny, nx, pieces)),
                dma((2, ny, nx, pieces)),
            ],
            compiler_params=pltpu.CompilerParams(
                collective_id=0, has_side_effects=True, vmem_limit_bytes=20 * 1024 * 1024
            ),
        )(
            *(
                pltpu.with_memory_space_constraint(a, pltpu.HBM)
                for a in (weight_gate, smooth_gate, weight_up, smooth_up, norm_train[None], norm_step[None])
            ),
        )
        serve_gate, serve_up, factor_gate, factor_up, norm_all, whole_gate, whole_up = store(
            landed, ((n_shard * rows, cols),) * 2 + tuple(a.shape for a in landed[2:])
        )
        serve_norm = norm_all[:, :, 0, :per].reshape(-1).astype(jnp.bfloat16)
        return (
            serve_gate, serve_up, factor_gate.reshape(-1), factor_up.reshape(-1),
            serve_norm, whole_gate, whole_up,
        )

    in_specs = (P("shard", "model"),) * 4 + (P(("shard", "model")),) * 2
    out_specs = (
        P(None, "model"),
        P(None, "model"),
        P("model"),
        P("model"),
        P(),
        P("shard", "model"),
        P("shard", "model"),
    )
    return jax.shard_map(body, mesh=mesh, in_specs=in_specs, out_specs=out_specs, check_vma=False)
```

profile of v0, /device:TPU:0, one launch (start us, length us, event | category | flops | bytes accessed | tf_op | source)
XLA Modules:
  0.0 131.1 jit_solution(16203629532192800367)
XLA Ops:
  0.6 118.4 %shard_map.117 = (bf16[4,3072,512]{2,1,0:T(8,128)(2,1)S(1)}, bf16[4,3072,512]{2,1,0:T(8,128)(2,1)S(1)}, f32[1,2048]{1,0:T(1,128)S(1)}, f32[1,2048]{1,0:T(1,128)S...) custom-call(f32[384,2048]{1,0:T(8,128)} %weight_gate.1, ...), custom_call_target="tpu_custom_call" | custom-call | tf_op jit(solution)/shard_map/pallas_call | solution.py:253
  119.1 10.5 %shard_map.118 = (bf16[3072,2048]{1,0:T(8,128)(2,1)}, bf16[3072,2048]{1,0:T(8,128)(2,1)}, f32[1,2048]{1,0:T(1,128)}, f32[1,2048]{1,0:T(1,128)}, f32[8,4,1,128]{3...) custom-call(bf16[4,3072,512]{2,1,0:T(8,128)(2,1)S(1)} %get-tuple-element.21.refs_0_, ...), custom_call_target="tpu_custom_call" | custom-call | tf_op jit(solution)/shard_map/pallas_call | solution.py:230
  129.6 0.8 fusion
  130.4 0.7 convert_element_type.4
where the time goes:
time: 131 us
  Pallas kernels  129 us (98%)
  local copies, waits for them, and re-layouts  1.45 us (1%)
    pallas_call x1, Pallas kernels, body(): pl.pallas_call(functools.partial(kernel, n_shard, n_model, ny, nx, pieces...  118 us
    pallas_call x1, Pallas kernels, store(): pl.pallas_call(functools.partial(store_kernel, len(arrays)), out_shape=tu...  10.5 us

commit v1 on v0

v1 whole, which is shorter than its diff:
```python
import functools
import math

import jax
import jax.numpy as jnp
from jax import lax
from jax.experimental import pallas as pl
from jax.experimental.pallas import tpu as pltpu
from jax.sharding import PartitionSpec as P

MESH = pl.DeviceIdType.MESH
keep_rate = 0.7
LANES = 128


def grid_of(n_shard):
    chips = n_shard // 2
    nx = math.isqrt(chips)
    while chips % nx:
        nx -= 1
    return chips // nx, nx


def widths_of(tiles, unit):
    if tiles < 4:
        return [1] * tiles
    if unit == 0:
        return [1, 2, tiles - 3]
    return [tiles // 2, tiles - tiles // 2 - 1, 1]


def pieces_of(cols):
    tiles = cols // LANES
    found = []
    for unit in range(2):
        queues = [(True, widths_of((tiles + 1) // 2, unit)), (False, widths_of(tiles // 2, unit))]
        at = 0
        for n in range(max(len(q) for _, q in queues)):
            for along_x, queue in queues:
                if n < len(queue):
                    found.append((unit, at * LANES, queue[n] * LANES, along_x, unit == 0 and n == 0))
                    at += queue[n]
    return found


def kernel(
    n_shard, n_model, ny, nx, pieces,
    weight_gate, smooth_gate, weight_up, smooth_up, norm_train, norm_step,
    serve_gate, serve_up, factor_gate, factor_up, norm_out, whole_gate, whole_up,
    weights, smooths, peaks, early, norm_in, norm_all, norm_rows,
    load_sem, norm_load, peak_send, peak_recv, norm_send, norm_recv, row_send, row_recv,
    x_send, y_send, pair_send, ring_recv, pair_recv,
):
    me = lax.axis_index("shard")
    col = lax.axis_index("model")
    core = lax.rem(me, 2)
    chip = me // 2
    xpos, ypos = lax.rem(chip, nx), chip // nx
    x_next = (ypos * nx + lax.rem(xpos + 1, nx)) * 2 + core
    y_next = (lax.rem(ypos + 1, ny) * nx + xpos) * 2 + core
    pair = chip * 2 + (1 - core)
    rows, cols = whole_gate.shape
    serves, wholes, factors = (serve_gate, serve_up), (whole_gate, whole_up), (factor_gate, factor_up)
    count = len(pieces)
    order = range(count)
    early_pieces = [p for p in order if pieces[p][4]]
    first = len(early_pieces)

    def across(p):
        return pl.ds(pieces[p][1], pieces[p][2])

    sources = ((weight_gate, smooth_gate), (weight_up, smooth_up))
    loads = {}
    for p in order:
        unit = pieces[p][0]
        for which, dst in enumerate((weights, smooths)):
            copy = pltpu.make_async_copy(
                sources[unit][which].at[:, across(p)], dst.at[unit, :, across(p)], load_sem.at[p, which]
            )
            copy.start()
            loads[p, which] = copy
        if p == first:
            norm_loads = [
                pltpu.make_async_copy(src, norm_in.at[i], norm_load.at[i])
                for i, src in enumerate((norm_train, norm_step))
            ]
            for copy in norm_loads:
                copy.start()

    barrier = pltpu.get_barrier_semaphore()
    for d in range(1, n_shard):
        pl.semaphore_signal(barrier, inc=1, device_id=(lax.rem(me + d, n_shard), col), device_id_type=MESH)
    for d in range(1, n_model):
        pl.semaphore_signal(barrier, inc=1, device_id=(me, lax.rem(col + d, n_model)), device_id_type=MESH)

    def average(p):
        unit, _, width = pieces[p][:3]
        for which in range(2):
            loads[p, which].wait()

        def step(i, top):
            span = pl.ds(pl.multiple_of(i * 8, 8), 8)
            value = keep_rate * smooths[unit, span, across(p)] + (1.0 - keep_rate) * weights[unit, span, across(p)]
            wholes[unit][span, across(p)] = value
            return jnp.maximum(top, jnp.abs(value))

        top = lax.fori_loop(0, rows // 8, step, jnp.zeros((8, width), jnp.float32), unroll=4)
        peaks[unit, me, :, across(p)] = jnp.max(top, axis=0, keepdims=True)

    peak_copies = {}

    def send_peaks(p):
        unit = pieces[p][0]
        peak_copies[p] = []
        for d in range(1, n_shard):
            ref = peaks.at[unit, me, :, across(p)]
            copy = pltpu.make_async_remote_copy(
                src_ref=ref, dst_ref=ref,
                send_sem=peak_send.at[p, d - 1], recv_sem=peak_recv.at[p, d - 1],
                device_id=(lax.rem(me + d, n_shard), col), device_id_type=MESH,
            )
            copy.start()
            peak_copies[p].append(copy)

    def piece_of(p, dy, dx, side):
        owner = (lax.rem(ypos - dy + ny, ny) * nx + lax.rem(xpos - dx + nx, nx)) * 2 + side
        return serves[pieces[p][0]].at[pl.ds(pl.multiple_of(owner * rows, rows), rows), across(p)]

    sent = []

    def start(src, dst, device, send_sem, recv_sem):
        copy = pltpu.make_async_remote_copy(
            src_ref=src, dst_ref=dst, send_sem=send_sem, recv_sem=recv_sem,
            device_id=(device, col), device_id_type=MESH,
        )
        copy.start()
        sent.append(copy)

    def along_x_first(p):
        return pieces[p][3]

    def to_x(p, dy, dx):
        if dx < nx - 1 and (dy == 0 or not along_x_first(p)):
            ref = piece_of(p, dy, dx, core)
            start(ref, ref, x_next, x_send.at[dy, dx, p], ring_recv.at[dy, dx + 1, p])

    def to_y(p, dy, dx):
        if dy < ny - 1 and (dx == 0 or along_x_first(p)):
            ref = piece_of(p, dy, dx, core)
            start(ref, ref, y_next, y_send.at[dy, dx, p], ring_recv.at[dy + 1, dx, p])

    def to_pair(p, dy, dx):
        ref = piece_of(p, dy, dx, core)
        start(ref, ref, pair, pair_send.at[dy, dx, p], pair_recv.at[dy, dx, p])

    def first_way(p):
        (to_x if along_x_first(p) else to_y)(p, 0, 0)

    def second_way(p):
        (to_y if along_x_first(p) else to_x)(p, 0, 0)

    def send_early(p):
        src = wholes[pieces[p][0]].at[:, across(p)]
        if along_x_first(p):
            if nx > 1:
                start(src, early.at[p], x_next, x_send.at[0, 0, p], ring_recv.at[0, 1, p])
        elif ny > 1:
            start(src, early.at[p], y_next, y_send.at[0, 0, p], ring_recv.at[1, 0, p])

    def landed_early(p, dy, dx):
        return pieces[p][4] and (dy, dx) == ((0, 1) if along_x_first(p) else (1, 0))

    def find_factor(p):
        unit = pieces[p][0]
        for copy in peak_copies[p]:
            copy.wait_recv()
        factor = peaks[unit, 0, :, across(p)]
        for d in range(1, n_shard):
            factor = jnp.maximum(factor, peaks[unit, d, :, across(p)])
        factors[unit][:, across(p)] = factor

    def narrow(p, owner, read):
        unit = pieces[p][0]

        def step(i, carry):
            at = i * 16
            value = read(pl.ds(pl.multiple_of(at, 16), 16)) / factors[unit][:, across(p)]
            serves[unit][pl.ds(pl.multiple_of(owner * rows + at, 16), 16), across(p)] = value.astype(jnp.bfloat16)
            return carry

        lax.fori_loop(0, rows // 16, step, 0, unroll=2)

    def narrow_own(p):
        narrow(p, me, lambda span: wholes[pieces[p][0]][span, across(p)])

    def arrived(p, dy, dx):
        if landed_early(p, dy, dx):
            ref = early.at[p]
            pltpu.make_async_copy(ref, ref, ring_recv.at[dy, dx, p]).wait()
            owner = (lax.rem(ypos - dy + ny, ny) * nx + lax.rem(xpos - dx + nx, nx)) * 2 + core
            narrow(p, owner, lambda span: early[p, span])
        else:
            ref = piece_of(p, dy, dx, core)
            pltpu.make_async_copy(ref, ref, ring_recv.at[dy, dx, p]).wait()

    per = norm_train.shape[1]
    lead = min(first + 2, count)
    for p in range(lead):
        average(p)
    pl.semaphore_wait(barrier, n_shard + n_model - 2)
    for p in range(lead):
        send_peaks(p)
    for p in early_pieces:
        send_early(p)
    for copy in norm_loads:
        copy.wait()
    norm_all[me, col, :, 0:per] = norm_in[0] + norm_in[1]
    for p in range(lead, count):
        average(p)
        if p > lead:
            send_peaks(p - 1)
    if count > lead:
        send_peaks(count - 1)
    norm_copies = []
    for d in range(1, n_model):
        copy = pltpu.make_async_remote_copy(
            src_ref=norm_all.at[me, col], dst_ref=norm_all.at[me, col],
            send_sem=norm_send.at[d - 1], recv_sem=norm_recv.at[d - 1],
            device_id=(me, lax.rem(col + d, n_model)), device_id_type=MESH,
        )
        copy.start()
        norm_copies.append(copy)

    row_copies = []

    def send_rows():
        for copy in norm_copies:
            copy.wait_recv()
        for d in range(1, n_shard):
            copy = pltpu.make_async_remote_copy(
                src_ref=norm_all.at[me], dst_ref=norm_all.at[me],
                send_sem=row_send.at[d - 1], recv_sem=row_recv.at[d - 1],
                device_id=(lax.rem(me + d, n_shard), col), device_id_type=MESH,
            )
            copy.start()
            row_copies.append(copy)

    before = None
    for p in range(first, count):
        find_factor(p)
        if before is not None:
            first_way(before)
        narrow_own(p)
        before = p
    for p in early_pieces:
        find_factor(p)
    if before is not None:
        first_way(before)
    send_rows()
    for p in early_pieces:
        narrow_own(p)
    for p in range(first, count):
        second_way(p)
    for p in early_pieces:
        second_way(p)
    for p in order:
        to_pair(p, 0, 0)

    def gather_norm():
        for copy in row_copies:
            copy.wait_recv()
        lane = lax.broadcasted_iota(jnp.int32, (8, LANES), 1)
        tiles = [jnp.zeros((8, LANES), jnp.float32) for _ in range(norm_out.shape[0])]
        for s in range(n_shard):
            for c in range(n_model):
                for at in range(0, per, LANES):
                    size = min(LANES, per - at)
                    tile, shift = divmod((s * n_model + c) * per + at, LANES)
                    row = jnp.broadcast_to(norm_all[s, c, :, at:at + LANES], (8, LANES))
                    if shift:
                        row = pltpu.roll(row, shift, 1)
                    tiles[tile] = jnp.where((lane >= shift) & (lane < shift + size), row, tiles[tile])
                    if shift + size > LANES:
                        tiles[tile + 1] = jnp.where(lane < shift + size - LANES, row, tiles[tile + 1])
        for t, tile in enumerate(tiles):
            norm_rows[t:t + 1] = tile[0:1]
        norm_out[...] = norm_rows[...].astype(jnp.bfloat16)

    for distance in range(1, ny + nx - 1):
        for own_way in (True, False):
            for p in order:
                for dy in range(ny):
                    dx = distance - dy
                    straight = (dy if along_x_first(p) else dx) == 0
                    if 0 <= dx < nx and straight == own_way:
                        arrived(p, dy, dx)
                        to_x(p, dy, dx)
                        to_y(p, dy, dx)
                        to_pair(p, dy, dx)
            if distance == 1 and own_way:
                gather_norm()

    for p in order:
        for dy in range(ny):
            for dx in range(nx):
                ref = piece_of(p, dy, dx, 1 - core)
                pltpu.make_async_copy(ref, ref, pair_recv.at[dy, dx, p]).wait()
    for copy in sent + sum(peak_copies.values(), []) + norm_copies + row_copies:
        copy.wait_send()


def store_kernel(count, parts, *refs):
    copies = []
    for src, dst in zip(refs[:count], refs[count:-1]):
        pieces = parts if src.shape[0] % (parts * 16) == 0 else 1
        size = src.shape[0] // pieces
        for n in range(pieces):
            span = pl.ds(n * size, size)
            copies.append(pltpu.make_async_copy(src.at[span], dst.at[span], refs[-1].at[len(copies)]))
            copies[-1].start()
    for copy in copies:
        copy.wait()


def store(arrays, parts):
    hbm = pl.BlockSpec(memory_space=pltpu.HBM)
    return pl.pallas_call(
        functools.partial(store_kernel, len(arrays), parts),
        out_shape=tuple(pltpu.HBM(a.shape, a.dtype) for a in arrays),
        in_specs=[pl.BlockSpec(memory_space=pltpu.VMEM)] * len(arrays),
        out_specs=(hbm,) * len(arrays),
        scratch_shapes=[pltpu.SemaphoreType.DMA((len(arrays) * parts,))],
        compiler_params=pltpu.CompilerParams(vmem_limit_bytes=1024 * 1024),
    )(*(pltpu.with_memory_space_constraint(a, pltpu.VMEM) for a in arrays))


def solution(mesh):
    n_shard, n_model = mesh.shape["shard"], mesh.shape["model"]
    ny, nx = grid_of(n_shard)

    def body(weight_gate, smooth_gate, weight_up, smooth_up, norm_train, norm_step):
        rows, cols = weight_gate.shape
        per = norm_train.shape[0]
        pieces = pieces_of(cols)
        count = len(pieces)
        wide = -(-per // LANES) * LANES
        width = n_shard * n_model * per
        tiles = -(-width // LANES)
        vmem = pl.BlockSpec(memory_space=pltpu.VMEM)
        hbm = pl.BlockSpec(memory_space=pltpu.HBM)
        dma = pltpu.SemaphoreType.DMA
        landed = pl.pallas_call(
            functools.partial(kernel, n_shard, n_model, ny, nx, pieces),
            out_shape=(
                pltpu.VMEM((n_shard * rows, cols), jnp.bfloat16),
                pltpu.VMEM((n_shard * rows, cols), jnp.bfloat16),
                pltpu.VMEM((1, cols), jnp.float32),
                pltpu.VMEM((1, cols), jnp.float32),
                pltpu.VMEM((tiles, LANES), jnp.bfloat16),
                pltpu.VMEM((rows, cols), jnp.float32),
                pltpu.VMEM((rows, cols), jnp.float32),
            ),
            in_specs=[hbm] * 6,
            out_specs=(vmem,) * 7,
            scratch_shapes=[
                pltpu.VMEM((2, rows, cols), jnp.float32),
                pltpu.VMEM((2, rows, cols), jnp.float32),
                pltpu.VMEM((2, n_shard, 1, cols), jnp.float32),
                pltpu.VMEM((2, rows, LANES), jnp.float32),
                pltpu.VMEM((2, 1, per), jnp.float32),
                pltpu.VMEM((n_shard, n_model, 1, wide), jnp.float32),
                pltpu.VMEM((tiles, LANES), jnp.float32),
                dma((count, 2)),
                dma((2,)),
                dma((count, n_shard)),
                dma((count, n_shard)),
                dma((n_model,)),
                dma((n_model,)),
                dma((n_shard,)),
                dma((n_shard,)),
                dma((ny, nx, count)),
                dma((ny, nx, count)),
                dma((ny, nx, count)),
                dma((ny, nx, count)),
                dma((ny, nx, count)),
            ],
            compiler_params=pltpu.CompilerParams(
                collective_id=0, has_side_effects=True, vmem_limit_bytes=20 * 1024 * 1024
            ),
        )(
            *(
                pltpu.with_memory_space_constraint(a, pltpu.HBM)
                for a in (weight_gate, smooth_gate, weight_up, smooth_up, norm_train[None], norm_step[None])
            ),
        )
        serve_gate, serve_up, factor_gate, factor_up, norm, whole_gate, whole_up = store(landed, 4)
        return (
            serve_gate, serve_up, factor_gate.reshape(-1), factor_up.reshape(-1),
            norm.reshape(-1)[:width], whole_gate, whole_up,
        )

    in_specs = (P("shard", "model"),) * 4 + (P(("shard", "model")),) * 2
    out_specs = (
        P(None, "model"),
        P(None, "model"),
        P("model"),
        P("model"),
        P(),
        P("shard", "model"),
        P("shard", "model"),
    )
    return jax.shard_map(body, mesh=mesh, in_specs=in_specs, out_specs=out_specs, check_vma=False)
```

time: 131 us -> 132 us (level)
  Pallas kernels: 129 us -> 131 us
  local copies, waits for them, and re-layouts: 1.45 us -> 0 us
    pallas_call x1, Pallas kernels: 118 us -> 120 us  [body(): pl.pallas_call(functools.partial(kernel, n_shard, n_model, ny, nx, pieces...]
where the time goes in v1:
time: 132 us; the launch traced here: 131 us
  Pallas kernels  131 us (99%)
    pallas_call x1, Pallas kernels, body(): pl.pallas_call(functools.partial(kernel, n_shard, n_model, ny, nx, pieces...  120 us
    pallas_call x1, Pallas kernels, store(): pl.pallas_call(functools.partial(store_kernel, len(arrays), parts), out_s...  10.5 us

profile of v1, /device:TPU:0, one launch (start us, length us, event | category | flops | bytes accessed | tf_op | source)
XLA Modules:
  0.0 131.4 jit_solution(1933484795393298656)
XLA Ops:
  0.6 120.2 %shard_map.117 = (bf16[3072,2048]{1,0:T(8,128)(2,1)S(1)}, bf16[3072,2048]{1,0:T(8,128)(2,1)S(1)}, f32[1,2048]{1,0:T(1,128)S(1)}, f32[1,2048]{1,0:T(1,128)S(1)}, ...) custom-call(f32[384,2048]{1,0:T(8,128)} %weight_gate.1, f32[384,2048]{1,0:T(8,128)} %smooth_gate.1, ...), custom_call_target="tpu_custom_call" | custom-call | tf_op jit(solution)/shard_map/pallas_call | solution.py:352
  120.8 10.5 %shard_map.118 = (bf16[3072,2048]{1,0:T(8,128)(2,1)}, bf16[3072,2048]{1,0:T(8,128)(2,1)}, f32[1,2048]{1,0:T(1,128)}, f32[1,2048]{1,0:T(1,128)}, bf16[24,128]{1,0...) custom-call(bf16[3072,2048]{1,0:T(8,128)(2,1)S(1)} %get-tuple-element.21.refs_0_, ...), custom_call_target="tpu_custom_call" | custom-call | tf_op jit(solution)/shard_map/pallas_call | solution.py:327

commit v2 on v1

v2 whole, which is shorter than its diff:
```python
import functools
import math

import jax
import jax.numpy as jnp
from jax import lax
from jax.experimental import pallas as pl
from jax.experimental.pallas import tpu as pltpu
from jax.sharding import PartitionSpec as P

MESH = pl.DeviceIdType.MESH
keep_rate = 0.7
LANES = 128


def grid_of(n_shard):
    chips = n_shard // 2
    nx = math.isqrt(chips)
    while chips % nx:
        nx -= 1
    return chips // nx, nx


def widths_of(tiles, unit):
    if tiles < 4:
        return [1] * tiles
    if unit == 0:
        return [1, 2, tiles - 3]
    return [tiles // 2, tiles - tiles // 2 - 1, 1]


def pieces_of(cols, early):
    tiles = cols // LANES
    found = []
    for unit in range(2):
        queues = [(True, widths_of((tiles + 1) // 2, unit)), (False, widths_of(tiles // 2, unit))]
        at = 0
        for n in range(max(len(q) for _, q in queues)):
            for along_x, queue in queues:
                if n < len(queue):
                    found.append((unit, at * LANES, queue[n] * LANES, along_x, early and unit == 0 and n == 0))
                    at += queue[n]
    return found


def kernel(
    n_shard, n_model, ny, nx, pieces,
    weight_gate, smooth_gate, weight_up, smooth_up, norm_train, norm_step,
    serve_gate, serve_up, factor_gate, factor_up, norm_out, whole_gate, whole_up,
    inputs, peaks, early, norm_in, norm_all, norm_rows,
    load_sem, peak_recv, ring_recv, pair_recv, sent_sem, small_sem,
):
    me = lax.axis_index("shard")
    col = lax.axis_index("model")
    core = lax.rem(me, 2)
    chip = me // 2
    xpos, ypos = lax.rem(chip, nx), chip // nx
    x_next = (ypos * nx + lax.rem(xpos + 1, nx)) * 2 + core
    y_next = (lax.rem(ypos + 1, ny) * nx + xpos) * 2 + core
    pair = chip * 2 + (1 - core)
    rows, cols = whole_gate.shape
    serves, wholes, factors = (serve_gate, serve_up), (whole_gate, whole_up), (factor_gate, factor_up)
    count = len(pieces)
    order = range(count)
    early_pieces = [p for p in order if pieces[p][4]]
    first = len(early_pieces)

    def across(p):
        return pl.ds(pieces[p][1], pieces[p][2])

    sources = ((weight_gate, smooth_gate), (weight_up, smooth_up))
    norm_load, norm_send, norm_recv, row_send, row_recv, peak_send = [small_sem.at[i] for i in range(6)]

    def wait_bytes(ref, sem):
        pltpu.make_async_copy(ref, ref, sem).wait()

    for p in order:
        unit = pieces[p][0]
        for which in range(2):
            pltpu.make_async_copy(
                sources[unit][which].at[:, across(p)], inputs.at[which, unit, :, across(p)], load_sem.at[p]
            ).start()
        if p == first:
            for i, src in enumerate((norm_train, norm_step)):
                pltpu.make_async_copy(src, norm_in.at[i], norm_load).start()

    barrier = pltpu.get_barrier_semaphore()
    for d in range(1, n_shard):
        pl.semaphore_signal(barrier, inc=1, device_id=(lax.rem(me + d, n_shard), col), device_id_type=MESH)
    for d in range(1, n_model):
        pl.semaphore_signal(barrier, inc=1, device_id=(me, lax.rem(col + d, n_model)), device_id_type=MESH)

    def average(p):
        unit, _, width = pieces[p][:3]
        wait_bytes(inputs.at[:, unit, :, across(p)], load_sem.at[p])

        def step(i, top):
            span = pl.ds(pl.multiple_of(i * 8, 8), 8)
            value = keep_rate * inputs[1, unit, span, across(p)] + (1.0 - keep_rate) * inputs[0, unit, span, across(p)]
            wholes[unit][span, across(p)] = value
            return jnp.maximum(top, jnp.abs(value))

        top = lax.fori_loop(0, rows // 8, step, jnp.zeros((8, width), jnp.float32), unroll=4)
        peaks[unit, me, :, across(p)] = jnp.max(top, axis=0, keepdims=True)

    def start(src, dst, device, send_sem, recv_sem):
        pltpu.make_async_remote_copy(
            src_ref=src, dst_ref=dst, send_sem=send_sem, recv_sem=recv_sem,
            device_id=device, device_id_type=MESH,
        ).start()

    def send_peaks(p):
        ref = peaks.at[pieces[p][0], me, :, across(p)]
        for d in range(1, n_shard):
            start(ref, ref, (lax.rem(me + d, n_shard), col), peak_send, peak_recv.at[p])

    def piece_of(p, dy, dx, side):
        owner = (lax.rem(ypos - dy + ny, ny) * nx + lax.rem(xpos - dx + nx, nx)) * 2 + side
        return serves[pieces[p][0]].at[pl.ds(pl.multiple_of(owner * rows, rows), rows), across(p)]

    def group_of(p):
        return 2 if pieces[p][4] else pieces[p][0]

    spots = [(dy, dx) for dy in range(ny) for dx in range(nx)][1:]

    def landing(p, dy, dx):
        return ring_recv.at[p * len(spots) + spots.index((dy, dx))]

    def along_x_first(p):
        return pieces[p][3]

    def to_x(p, dy, dx):
        if dx < nx - 1 and (dy == 0 or not along_x_first(p)):
            ref = piece_of(p, dy, dx, core)
            start(ref, ref, (x_next, col), sent_sem.at[group_of(p)], landing(p, dy, dx + 1))

    def to_y(p, dy, dx):
        if dy < ny - 1 and (dx == 0 or along_x_first(p)):
            ref = piece_of(p, dy, dx, core)
            start(ref, ref, (y_next, col), sent_sem.at[group_of(p)], landing(p, dy + 1, dx))

    def to_pair(p, dy, dx):
        ref = piece_of(p, dy, dx, core)
        start(ref, ref, (pair, col), sent_sem.at[group_of(p)], pair_recv.at[pieces[p][0]])

    def first_way(p):
        (to_x if along_x_first(p) else to_y)(p, 0, 0)

    def second_way(p):
        (to_y if along_x_first(p) else to_x)(p, 0, 0)

    def send_early(p):
        src = wholes[pieces[p][0]].at[:, across(p)]
        if along_x_first(p):
            start(src, early.at[p], (x_next, col), sent_sem.at[3 + p], landing(p, 0, 1))
        else:
            start(src, early.at[p], (y_next, col), sent_sem.at[3 + p], landing(p, 1, 0))

    def landed_early(p, dy, dx):
        return pieces[p][4] and (dy, dx) == ((0, 1) if along_x_first(p) else (1, 0))

    def find_factor(p):
        unit = pieces[p][0]
        wait_bytes(peaks.at[unit, pl.ds(0, n_shard - 1), :, across(p)], peak_recv.at[p])
        factor = peaks[unit, 0, :, across(p)]
        for d in range(1, n_shard):
            factor = jnp.maximum(factor, peaks[unit, d, :, across(p)])
        factors[unit][:, across(p)] = factor

    def narrow(p, owner, read):
        unit = pieces[p][0]

        def step(i, carry):
            at = i * 16
            value = read(pl.ds(pl.multiple_of(at, 16), 16)) / factors[unit][:, across(p)]
            serves[unit][pl.ds(pl.multiple_of(owner * rows + at, 16), 16), across(p)] = value.astype(jnp.bfloat16)
            return carry

        lax.fori_loop(0, rows // 16, step, 0, unroll=2)

    def narrow_own(p):
        narrow(p, me, lambda span: wholes[pieces[p][0]][span, across(p)])

    def arrived(p, dy, dx):
        if landed_early(p, dy, dx):
            wait_bytes(early.at[p], landing(p, dy, dx))
            owner = (lax.rem(ypos - dy + ny, ny) * nx + lax.rem(xpos - dx + nx, nx)) * 2 + core
            narrow(p, owner, lambda span: early[p, span])
        else:
            wait_bytes(piece_of(p, dy, dx, core), landing(p, dy, dx))

    per = norm_train.shape[1]
    lead = min(first + 2, count)
    for p in range(lead):
        average(p)
    pl.semaphore_wait(barrier, n_shard + n_model - 2)
    for p in range(lead):
        send_peaks(p)
    for p in early_pieces:
        send_early(p)
    wait_bytes(norm_in, norm_load)
    norm_all[me, col, :, 0:per] = norm_in[0] + norm_in[1]
    for p in range(lead, count):
        average(p)
        if p > lead:
            send_peaks(p - 1)
    if count > lead:
        send_peaks(count - 1)
    for d in range(1, n_model):
        ref = norm_all.at[me, col]
        start(ref, ref, (me, lax.rem(col + d, n_model)), norm_send, norm_recv)

    late = list(range(first, count))
    for p in late[:2]:
        find_factor(p)
    for n, p in enumerate(late[:2]):
        narrow_own(p)
        if n < first:
            find_factor(n)
        first_way(p)
    for p in early_pieces[len(late[:2]):]:
        find_factor(p)
    wait_bytes(norm_all.at[0, pl.ds(0, n_model - 1)], norm_recv)
    for d in range(1, n_shard):
        start(norm_all.at[me], norm_all.at[me], (lax.rem(me + d, n_shard), col), row_send, row_recv)
    before = None
    for p in late[2:]:
        find_factor(p)
        if before is not None:
            first_way(before)
        narrow_own(p)
        before = p
    for p in early_pieces:
        narrow_own(p)
    if before is not None:
        first_way(before)
    for p in late + early_pieces:
        second_way(p)
    for p in order:
        to_pair(p, 0, 0)

    def gather_norm():
        wait_bytes(norm_all.at[pl.ds(0, n_shard - 1)], row_recv)
        lane = lax.broadcasted_iota(jnp.int32, (8, LANES), 1)
        tiles = [jnp.zeros((8, LANES), jnp.float32) for _ in range(norm_out.shape[0])]
        for s in range(n_shard):
            for c in range(n_model):
                for at in range(0, per, LANES):
                    size = min(LANES, per - at)
                    tile, shift = divmod((s * n_model + c) * per + at, LANES)
                    row = jnp.broadcast_to(norm_all[s, c, :, at:at + LANES], (8, LANES))
                    if shift:
                        row = pltpu.roll(row, shift, 1)
                    tiles[tile] = jnp.where((lane >= shift) & (lane < shift + size), row, tiles[tile])
                    if shift + size > LANES:
                        tiles[tile + 1] = jnp.where(lane < shift + size - LANES, row, tiles[tile + 1])
        for t, tile in enumerate(tiles):
            norm_rows[t:t + 1] = tile[0:1]
        norm_out[...] = norm_rows[...].astype(jnp.bfloat16)

    for distance in range(1, ny + nx - 1):
        for own_way in (True, False):
            for p in order:
                for dy in range(ny):
                    dx = distance - dy
                    straight = (dy if along_x_first(p) else dx) == 0
                    if 0 <= dx < nx and straight == own_way:
                        arrived(p, dy, dx)
                        to_x(p, dy, dx)
                        to_y(p, dy, dx)
                        to_pair(p, dy, dx)
            if distance == 1 and own_way:
                gather_norm()

    spread = first * LANES
    hops = 2 * ny * nx - 1
    for unit in range(2):
        wait_bytes(serves[unit].at[pl.ds(0, ny * nx * rows)], pair_recv.at[unit])
    wait_bytes(serve_gate.at[pl.ds(0, hops * rows), pl.ds(spread, cols - spread)], sent_sem.at[0])
    wait_bytes(serve_up.at[pl.ds(0, hops * rows)], sent_sem.at[1])
    if early_pieces:
        wait_bytes(serve_gate.at[pl.ds(0, (hops - 1) * rows), pl.ds(0, spread)], sent_sem.at[2])
    for p in early_pieces:
        wait_bytes(early.at[p], sent_sem.at[3 + p])
    wait_bytes(peaks.at[:, pl.ds(0, n_shard - 1)], peak_send)
    wait_bytes(norm_all.at[0, pl.ds(0, n_model - 1)], norm_send)
    wait_bytes(norm_all.at[pl.ds(0, n_shard - 1)], row_send)


def store_kernel(count, parts, *refs):
    pairs = list(zip(refs[:count], refs[count:-1]))
    for n, (src, dst) in enumerate(pairs):
        pieces = parts if src.shape[0] % (parts * 16) == 0 else 1
        size = src.shape[0] // pieces
        for part in range(pieces):
            span = pl.ds(part * size, size)
            pltpu.make_async_copy(src.at[span], dst.at[span], refs[-1].at[n]).start()
    for n, (src, dst) in enumerate(pairs):
        pltpu.make_async_copy(src, dst, refs[-1].at[n]).wait()


def store(arrays, parts):
    hbm = pl.BlockSpec(memory_space=pltpu.HBM)
    return pl.pallas_call(
        functools.partial(store_kernel, len(arrays), parts),
        out_shape=tuple(pltpu.HBM(a.shape, a.dtype) for a in arrays),
        in_specs=[pl.BlockSpec(memory_space=pltpu.VMEM)] * len(arrays),
        out_specs=(hbm,) * len(arrays),
        scratch_shapes=[pltpu.SemaphoreType.DMA((len(arrays),))],
        compiler_params=pltpu.CompilerParams(vmem_limit_bytes=1024 * 1024),
    )(*(pltpu.with_memory_space_constraint(a, pltpu.VMEM) for a in arrays))


def solution(mesh):
    n_shard, n_model = mesh.shape["shard"], mesh.shape["model"]
    ny, nx = grid_of(n_shard)

    def body(weight_gate, smooth_gate, weight_up, smooth_up, norm_train, norm_step):
        rows, cols = weight_gate.shape
        per = norm_train.shape[0]
        pieces = pieces_of(cols, min(nx, ny) > 1)
        count = len(pieces)
        wide = -(-per // LANES) * LANES
        width = n_shard * n_model * per
        tiles = -(-width // LANES)
        vmem = pl.BlockSpec(memory_space=pltpu.VMEM)
        hbm = pl.BlockSpec(memory_space=pltpu.HBM)
        dma = pltpu.SemaphoreType.DMA
        landed = pl.pallas_call(
            functools.partial(kernel, n_shard, n_model, ny, nx, pieces),
            out_shape=(
                pltpu.VMEM((n_shard * rows, cols), jnp.bfloat16),
                pltpu.VMEM((n_shard * rows, cols), jnp.bfloat16),
                pltpu.VMEM((1, cols), jnp.float32),
                pltpu.VMEM((1, cols), jnp.float32),
                pltpu.VMEM((tiles, LANES), jnp.bfloat16),
                pltpu.VMEM((rows, cols), jnp.float32),
                pltpu.VMEM((rows, cols), jnp.float32),
            ),
            in_specs=[hbm] * 6,
            out_specs=(vmem,) * 7,
            scratch_shapes=[
                pltpu.VMEM((2, 2, rows, cols), jnp.float32),
                pltpu.VMEM((2, n_shard, 1, cols), jnp.float32),
                pltpu.VMEM((2, rows, LANES), jnp.float32),
                pltpu.VMEM((2, 1, per), jnp.float32),
                pltpu.VMEM((n_shard, n_model, 1, wide), jnp.float32),
                pltpu.VMEM((tiles, LANES), jnp.float32),
                dma((count,)),
                dma((count,)),
                dma((count * (ny * nx - 1),)),
                dma((2,)),
                dma((5,)),
                dma((6,)),
            ],
            compiler_params=pltpu.CompilerParams(
                collective_id=0, has_side_effects=True, vmem_limit_bytes=20 * 1024 * 1024
            ),
        )(
            *(
                pltpu.with_memory_space_constraint(a, pltpu.HBM)
                for a in (weight_gate, smooth_gate, weight_up, smooth_up, norm_train[None], norm_step[None])
            ),
        )
        serve_gate, serve_up, factor_gate, factor_up, norm, whole_gate, whole_up = store(landed, 4)
        return (
            serve_gate, serve_up, factor_gate.reshape(-1), factor_up.reshape(-1),
            norm.reshape(-1)[:width], whole_gate, whole_up,
        )

    in_specs = (P("shard", "model"),) * 4 + (P(("shard", "model")),) * 2
    out_specs = (
        P(None, "model"),
        P(None, "model"),
        P("model"),
        P("model"),
        P(),
        P("shard", "model"),
        P("shard", "model"),
    )
    return jax.shard_map(body, mesh=mesh, in_specs=in_specs, out_specs=out_specs, check_vma=False)
```

time: 132 us -> 125 us (0.947)
  Pallas kernels: 131 us -> 124 us
    pallas_call x1, Pallas kernels: 120 us -> 114 us  [body(): pl.pallas_call(functools.partial(kernel, n_shard, n_model, ny, nx, pieces...]
where the time goes in v2:
time: 125 us
  Pallas kernels  124 us (99%)
    pallas_call x1, Pallas kernels, body(): pl.pallas_call(functools.partial(kernel, n_shard, n_model, ny, nx, pieces...  114 us
    pallas_call x1, Pallas kernels, store(): pl.pallas_call(functools.partial(store_kernel, len(arrays), parts), out_s...  10.4 us

profile of v2, /device:TPU:0, one launch (start us, length us, event | category | flops | bytes accessed | tf_op | source)
XLA Modules:
  0.0 124.7 jit_solution(10831435379662795471)
XLA Ops:
  0.6 113.7 %shard_map.117 = (bf16[3072,2048]{1,0:T(8,128)(2,1)S(1)}, bf16[3072,2048]{1,0:T(8,128)(2,1)S(1)}, f32[1,2048]{1,0:T(1,128)S(1)}, f32[1,2048]{1,0:T(1,128)S(1)}, ...) custom-call(f32[384,2048]{1,0:T(8,128)} %weight_gate.1, f32[384,2048]{1,0:T(8,128)} %smooth_gate.1, ...), custom_call_target="tpu_custom_call" | custom-call | tf_op jit(solution)/shard_map/pallas_call | solution.py:329
  114.4 10.4 %shard_map.118 = (bf16[3072,2048]{1,0:T(8,128)(2,1)}, bf16[3072,2048]{1,0:T(8,128)(2,1)}, f32[1,2048]{1,0:T(1,128)}, f32[1,2048]{1,0:T(1,128)}, bf16[24,128]{1,0...) custom-call(bf16[3072,2048]{1,0:T(8,128)(2,1)S(1)} %get-tuple-element.21.refs_0_, ...), custom_call_target="tpu_custom_call" | custom-call | tf_op jit(solution)/shard_map/pallas_call | solution.py:304

commit v3 on v2

v3 whole, which is shorter than its diff:
```python
import functools
import math

import jax
import jax.numpy as jnp
from jax import lax
from jax.experimental import pallas as pl
from jax.experimental.pallas import tpu as pltpu
from jax.sharding import PartitionSpec as P

MESH = pl.DeviceIdType.MESH
keep_rate = 0.7
LANES = 128


def grid_of(n_shard):
    chips = n_shard // 2
    nx = math.isqrt(chips)
    while chips % nx:
        nx -= 1
    return chips // nx, nx


def pieces_of(cols, early):
    tiles = cols // LANES
    found = []
    for unit in range(2):
        queues = []
        for along_x, many in ((True, (tiles + 1) // 2), (False, tiles // 2)):
            if many < 3:
                widths = [1] * many
            else:
                widths = [1, 1, many - 2] if unit == 0 else [many - 1, 1]
            queues.append((along_x, widths))
        at = 0
        for n in range(max(len(q) for _, q in queues)):
            for along_x, widths in queues:
                if n < len(widths):
                    found.append((unit, at * LANES, widths[n] * LANES, along_x, early and unit == 0 and n == 1))
                    at += widths[n]
    return found


def spans_of(pieces):
    spans = []
    for unit, at, width, _, _ in pieces:
        if spans and spans[-1][0] == unit and spans[-1][2] + width <= 2 * LANES:
            spans[-1] = (unit, spans[-1][1], spans[-1][2] + width)
        else:
            spans.append((unit, at, width))
    return spans


def kernel(
    n_shard, n_model, ny, nx, pieces, spans,
    weight_gate, smooth_gate, weight_up, smooth_up, norm_train, norm_step,
    serve_gate, serve_up, factor_gate, factor_up, norm_out, whole_gate, whole_up,
    inputs, peaks, early, norm_in, norm_mine, norm_all, norm_rows,
    load_sem, peak_recv, ring_recv, second_recv, pair_recv, sent_sem, small_sem,
):
    me = lax.axis_index("shard")
    col = lax.axis_index("model")
    core = lax.rem(me, 2)
    chip = me // 2
    xpos, ypos = lax.rem(chip, nx), chip // nx
    x_next = (ypos * nx + lax.rem(xpos + 1, nx)) * 2 + core
    y_next = (lax.rem(ypos + 1, ny) * nx + xpos) * 2 + core
    pair = chip * 2 + (1 - core)
    rows, cols = whole_gate.shape
    serves, wholes, factors = (serve_gate, serve_up), (whole_gate, whole_up), (factor_gate, factor_up)
    order = range(len(pieces))
    early_pieces = [p for p in order if pieces[p][4]]
    lead = 1
    is_lead = me == lead
    per = norm_train.shape[1]
    norm_load, peak_send, mine_send, mine_recv, z_send, z_recv, all_send, all_recv = [small_sem.at[i] for i in range(8)]

    def across(p):
        return pl.ds(pieces[p][1], pieces[p][2])

    def wait_bytes(ref, sem):
        pltpu.make_async_copy(ref, ref, sem).wait()

    groups = [[], [], []]
    for p in order:
        groups[2 if pieces[p][0] else int(pieces[p][1] >= 2 * LANES)].append(p)
    reach = [(pieces[g[0]][0], pieces[g[0]][1], sum(pieces[p][2] for p in g)) for g in groups if g]
    groups = [g for g in groups if g]

    sources = ((weight_gate, smooth_gate), (weight_up, smooth_up))
    for n, (unit, at, width) in enumerate(spans):
        for which in range(2):
            pltpu.make_async_copy(
                sources[unit][which].at[:, pl.ds(at, width)], inputs.at[which, unit, :, pl.ds(at, width)], load_sem.at[n]
            ).start()
    for i, src in enumerate((norm_train, norm_step)):
        pltpu.make_async_copy(src, norm_in.at[i], norm_load).start()

    barrier = pltpu.get_barrier_semaphore()
    for d in range(1, n_shard):
        pl.semaphore_signal(barrier, inc=1, device_id=(lax.rem(me + d, n_shard), col), device_id_type=MESH)

    @pl.when(is_lead)
    def _():
        for d in range(1, n_model):
            pl.semaphore_signal(barrier, inc=1, device_id=(me, lax.rem(col + d, n_model)), device_id_type=MESH)

    def average(n):
        unit, first, width = spans[n]
        here = pl.ds(first, width)
        wait_bytes(inputs.at[:, unit, :, here], load_sem.at[n])

        def step(i, top):
            rows_now = pl.ds(pl.multiple_of(i * 8, 8), 8)
            value = keep_rate * inputs[1, unit, rows_now, here] + (1.0 - keep_rate) * inputs[0, unit, rows_now, here]
            wholes[unit][rows_now, here] = value
            return jnp.maximum(top, jnp.abs(value))

        top = lax.fori_loop(0, rows // 8, step, jnp.zeros((8, width), jnp.float32), unroll=4)
        peaks[unit, me, :, here] = jnp.max(top, axis=0, keepdims=True)

    def start(src, dst, device, send_sem, recv_sem):
        pltpu.make_async_remote_copy(
            src_ref=src, dst_ref=dst, send_sem=send_sem, recv_sem=recv_sem,
            device_id=device, device_id_type=MESH,
        ).start()

    def send_peaks(g):
        unit, at, width = reach[g]
        ref = peaks.at[unit, me, :, pl.ds(at, width)]
        for d in range(1, n_shard):
            start(ref, ref, (lax.rem(me + d, n_shard), col), peak_send, peak_recv.at[g])

    def piece_of(p, dy, dx, side):
        owner = (lax.rem(ypos - dy + ny, ny) * nx + lax.rem(xpos - dx + nx, nx)) * 2 + side
        return serves[pieces[p][0]].at[pl.ds(pl.multiple_of(owner * rows, rows), rows), across(p)]

    def group_of(p):
        return 2 if pieces[p][4] else pieces[p][0]

    def along_x_first(p):
        return pieces[p][3]

    def on_second_way(p, dy, dx):
        return (dy, dx) == ((1, 0) if along_x_first(p) else (0, 1))

    landings = [(p, dy, dx) for p in order for dy in range(ny) for dx in range(nx)]
    landings = [spot for spot in landings if spot[1:] != (0, 0) and not on_second_way(*spot)]

    def landing(p, dy, dx):
        if on_second_way(p, dy, dx):
            return second_recv.at[pieces[p][0]]
        return ring_recv.at[landings.index((p, dy, dx))]

    def to_x(p, dy, dx):
        if dx < nx - 1 and (dy == 0 or not along_x_first(p)):
            ref = piece_of(p, dy, dx, core)
            start(ref, ref, (x_next, col), sent_sem.at[group_of(p)], landing(p, dy, dx + 1))

    def to_y(p, dy, dx):
        if dy < ny - 1 and (dx == 0 or along_x_first(p)):
            ref = piece_of(p, dy, dx, core)
            start(ref, ref, (y_next, col), sent_sem.at[group_of(p)], landing(p, dy + 1, dx))

    def to_pair(p, dy, dx):
        ref = piece_of(p, dy, dx, core)
        start(ref, ref, (pair, col), sent_sem.at[group_of(p)], pair_recv.at[pieces[p][0]])

    def first_way(p):
        (to_x if along_x_first(p) else to_y)(p, 0, 0)

    def second_way(p):
        (to_y if along_x_first(p) else to_x)(p, 0, 0)

    chunks = 4 if rows % 32 == 0 else 1

    def send_early(chunk):
        span = pl.ds(chunk * (rows // chunks), rows // chunks)
        for n, p in enumerate(early_pieces):
            device, spot = (x_next, (0, 1)) if along_x_first(p) else (y_next, (1, 0))
            start(
                wholes[pieces[p][0]].at[span, across(p)], early.at[n, span], (device, col),
                sent_sem.at[3 + n], landing(p, *spot),
            )

    def landed_early(p, dy, dx):
        return pieces[p][4] and (dy, dx) == ((0, 1) if along_x_first(p) else (1, 0))

    def find_factor(g):
        unit, at, width = reach[g]
        here = pl.ds(at, width)
        wait_bytes(peaks.at[unit, pl.ds(0, n_shard - 1), :, here], peak_recv.at[g])
        factor = peaks[unit, 0, :, here]
        for d in range(1, n_shard):
            factor = jnp.maximum(factor, peaks[unit, d, :, here])
        factors[unit][:, here] = factor

    def narrow(p, owner, read):
        unit = pieces[p][0]

        def step(i, carry):
            at = i * 16
            value = read(pl.ds(pl.multiple_of(at, 16), 16)) / factors[unit][:, across(p)]
            serves[unit][pl.ds(pl.multiple_of(owner * rows + at, 16), 16), across(p)] = value.astype(jnp.bfloat16)
            return carry

        lax.fori_loop(0, rows // 16, step, 0, unroll=2)

    def narrow_own(p):
        narrow(p, me, lambda span: wholes[pieces[p][0]][span, across(p)])

    seconds = set()

    def arrived(p, dy, dx):
        if landed_early(p, dy, dx):
            n = early_pieces.index(p)
            wait_bytes(early.at[n], landing(p, dy, dx))
            owner = (lax.rem(ypos - dy + ny, ny) * nx + lax.rem(xpos - dx + nx, nx)) * 2 + core
            narrow(p, owner, lambda span: early[n, span])
        elif not on_second_way(p, dy, dx):
            wait_bytes(piece_of(p, dy, dx, core), landing(p, dy, dx))
        elif pieces[p][0] not in seconds:
            seconds.add(pieces[p][0])
            wait_bytes(serves[pieces[p][0]].at[pl.ds(0, rows)], landing(p, dy, dx))

    def norm_sum():
        wait_bytes(norm_in, norm_load)
        norm_mine[...] = jnp.zeros(norm_mine.shape, jnp.float32)
        norm_mine[:, 0:per] = norm_in[0] + norm_in[1]

    def norm_to_lead():
        @pl.when(jnp.logical_not(is_lead))
        def _():
            start(norm_mine, norm_all.at[col, me], (lead, col), mine_send, mine_recv)

    def norm_spread():
        @pl.when(is_lead)
        def _():
            norm_all[col, me] = norm_mine[...]
            wait_bytes(norm_all.at[0, pl.ds(0, n_shard - 1)], mine_recv)
            for d in range(1, n_model):
                start(norm_all.at[col], norm_all.at[col], (me, lax.rem(col + d, n_model)), z_send, z_recv)
            wait_bytes(norm_all.at[pl.ds(0, n_model - 1)], z_recv)
            for d in range(1, n_shard):
                start(norm_all, norm_all, (lax.rem(me + d, n_shard), col), all_send, all_recv)

    average(0)

    @pl.when(is_lead)
    def _():
        pl.semaphore_wait(barrier, n_shard + n_model - 2)

    @pl.when(jnp.logical_not(is_lead))
    def _():
        pl.semaphore_wait(barrier, n_shard - 1)

    ends = [at + width for _, at, width in reach]
    ready, chunk = 0, 0
    for n, (unit, at, width) in enumerate(spans):
        if n:
            average(n)
        if (unit, at + width) == (reach[ready][0], ends[ready]):
            send_peaks(ready)
            ready += 1
        if n and chunk < chunks:
            send_early(chunk)
            chunk += 1
    while chunk < chunks:
        send_early(chunk)
        chunk += 1

    for g, group in enumerate(groups):
        find_factor(g)
        before = None
        for p in [p for p in group if p not in early_pieces] + [p for p in group if p in early_pieces]:
            narrow_own(p)
            if before is not None:
                first_way(before)
            before = None if p in early_pieces else p
        if g == 0:
            norm_sum()
        if g == len(groups) - 1:
            for p in groups[0]:
                to_pair(p, 0, 0)
        if before is not None:
            first_way(before)
        if g == 0:
            norm_to_lead()
    norm_spread()
    for p in order:
        if p not in early_pieces:
            second_way(p)
    for p in early_pieces:
        second_way(p)
    for group in groups[1:]:
        for p in group:
            to_pair(p, 0, 0)

    def gather_norm():
        @pl.when(jnp.logical_not(is_lead))
        def _():
            wait_bytes(norm_all, all_recv)

        lane = lax.broadcasted_iota(jnp.int32, (8, LANES), 1)
        tiles = [jnp.zeros((8, LANES), jnp.float32) for _ in range(norm_out.shape[0])]
        for s in range(n_shard):
            for c in range(n_model):
                for at in range(0, per, LANES):
                    size = min(LANES, per - at)
                    tile, shift = divmod((s * n_model + c) * per + at, LANES)
                    row = jnp.broadcast_to(norm_all[c, s, :, at:at + LANES], (8, LANES))
                    if shift:
                        row = pltpu.roll(row, shift, 1)
                    tiles[tile] = jnp.where((lane >= shift) & (lane < shift + size), row, tiles[tile])
                    if shift + size > LANES:
                        tiles[tile + 1] = jnp.where(lane < shift + size - LANES, row, tiles[tile + 1])
        for t, tile in enumerate(tiles):
            norm_rows[t:t + 1] = tile[0:1]
        norm_out[...] = norm_rows[...].astype(jnp.bfloat16)

    for distance in range(1, ny + nx - 1):
        for own_way in (True, False):
            for p in order:
                for dy in range(ny):
                    dx = distance - dy
                    straight = (dy if along_x_first(p) else dx) == 0
                    if 0 <= dx < nx and straight == own_way:
                        arrived(p, dy, dx)
                        to_x(p, dy, dx)
                        to_y(p, dy, dx)
                        to_pair(p, dy, dx)
            if distance == 1 and own_way:
                gather_norm()

    spread = len(early_pieces) * LANES
    hops = 2 * ny * nx - 1
    for unit in range(2):
        wait_bytes(serves[unit].at[pl.ds(0, ny * nx * rows)], pair_recv.at[unit])
    wait_bytes(serve_gate.at[pl.ds(0, hops * rows), pl.ds(0, cols - spread)], sent_sem.at[0])
    wait_bytes(serve_up.at[pl.ds(0, hops * rows)], sent_sem.at[1])
    if early_pieces:
        wait_bytes(serve_gate.at[pl.ds(0, (hops - 1) * rows), pl.ds(0, spread)], sent_sem.at[2])
    for n in range(len(early_pieces)):
        wait_bytes(early.at[n], sent_sem.at[3 + n])
    wait_bytes(peaks.at[:, pl.ds(0, n_shard - 1)], peak_send)

    @pl.when(is_lead)
    def _():
        wait_bytes(norm_all.at[pl.ds(0, n_model - 1)], z_send)
        halves = (n_shard - 1) * math.prod(norm_all.shape) * 2
        wide = next(w for w in (LANES << k for k in range(16)) if halves // w <= n_shard * rows)
        wait_bytes(serve_gate.at[pl.ds(0, halves // wide), pl.ds(0, wide)], all_send)

    @pl.when(jnp.logical_not(is_lead))
    def _():
        wait_bytes(norm_mine, mine_send)


def store_kernel(count, parts, *refs):
    pairs = list(zip(refs[:count], refs[count:-1]))
    for n, (src, dst) in enumerate(pairs):
        pieces = parts if src.shape[0] % (parts * 16) == 0 else 1
        size = src.shape[0] // pieces
        for part in range(pieces):
            span = pl.ds(part * size, size)
            pltpu.make_async_copy(src.at[span], dst.at[span], refs[-1].at[n]).start()
    for n, (src, dst) in enumerate(pairs):
        pltpu.make_async_copy(src, dst, refs[-1].at[n]).wait()


def store(arrays, parts):
    hbm = pl.BlockSpec(memory_space=pltpu.HBM)
    return pl.pallas_call(
        functools.partial(store_kernel, len(arrays), parts),
        out_shape=tuple(pltpu.HBM(a.shape, a.dtype) for a in arrays),
        in_specs=[pl.BlockSpec(memory_space=pltpu.VMEM)] * len(arrays),
        out_specs=(hbm,) * len(arrays),
        scratch_shapes=[pltpu.SemaphoreType.DMA((len(arrays),))],
        compiler_params=pltpu.CompilerParams(vmem_limit_bytes=1024 * 1024),
    )(*(pltpu.with_memory_space_constraint(a, pltpu.VMEM) for a in arrays))


def solution(mesh):
    n_shard, n_model = mesh.shape["shard"], mesh.shape["model"]
    ny, nx = grid_of(n_shard)

    def body(weight_gate, smooth_gate, weight_up, smooth_up, norm_train, norm_step):
        rows, cols = weight_gate.shape
        per = norm_train.shape[0]
        pieces = pieces_of(cols, min(nx, ny) > 1)
        spans = spans_of(pieces)
        count = len(pieces)
        wide = -(-per // LANES) * LANES
        width = n_shard * n_model * per
        tiles = -(-width // LANES)
        vmem = pl.BlockSpec(memory_space=pltpu.VMEM)
        hbm = pl.BlockSpec(memory_space=pltpu.HBM)
        dma = pltpu.SemaphoreType.DMA
        landed = pl.pallas_call(
            functools.partial(kernel, n_shard, n_model, ny, nx, pieces, spans),
            out_shape=(
                pltpu.VMEM((n_shard * rows, cols), jnp.bfloat16),
                pltpu.VMEM((n_shard * rows, cols), jnp.bfloat16),
                pltpu.VMEM((1, cols), jnp.float32),
                pltpu.VMEM((1, cols), jnp.float32),
                pltpu.VMEM((tiles, LANES), jnp.bfloat16),
                pltpu.VMEM((rows, cols), jnp.float32),
                pltpu.VMEM((rows, cols), jnp.float32),
            ),
            in_specs=[hbm] * 6,
            out_specs=(vmem,) * 7,
            scratch_shapes=[
                pltpu.VMEM((2, 2, rows, cols), jnp.float32),
                pltpu.VMEM((2, n_shard, 1, cols), jnp.float32),
                pltpu.VMEM((2, rows, LANES), jnp.float32),
                pltpu.VMEM((2, 1, per), jnp.float32),
                pltpu.VMEM((1, wide), jnp.float32),
                pltpu.VMEM((n_model, n_shard, 1, wide), jnp.float32),
                pltpu.VMEM((tiles, LANES), jnp.float32),
                dma((len(spans),)),
                dma((3,)),
                dma((count * (ny * nx - 2),)),
                dma((2,)),
                dma((2,)),
                dma((5,)),
                dma((8,)),
            ],
            compiler_params=pltpu.CompilerParams(
                collective_id=0, has_side_effects=True, vmem_limit_bytes=20 * 1024 * 1024
            ),
        )(
            *(
                pltpu.with_memory_space_constraint(a, pltpu.HBM)
                for a in (weight_gate, smooth_gate, weight_up, smooth_up, norm_train[None], norm_step[None])
            ),
        )
        serve_gate, serve_up, factor_gate, factor_up, norm, whole_gate, whole_up = store(landed, 4)
        return (
            serve_gate, serve_up, factor_gate.reshape(-1), factor_up.reshape(-1),
            norm.reshape(-1)[:width], whole_gate, whole_up,
        )

    in_specs = (P("shard", "model"),) * 4 + (P(("shard", "model")),) * 2
    out_specs = (
        P(None, "model"),
        P(None, "model"),
        P("model"),
        P("model"),
        P(),
        P("shard", "model"),
        P("shard", "model"),
    )
    return jax.shard_map(body, mesh=mesh, in_specs=in_specs, out_specs=out_specs, check_vma=False)
```

time: 125 us -> 123 us (0.984)
    pallas_call x1, Pallas kernels: 114 us -> 112 us  [body(): pl.pallas_call(functools.partial(kernel, n_shard, n_model, ny, nx, pieces...]
where the time goes in v3:
time: 123 us
  Pallas kernels  123 us (100%)
    pallas_call x1, Pallas kernels, body(): pl.pallas_call(functools.partial(kernel, n_shard, n_model, ny, nx, pieces...  112 us
    pallas_call x1, Pallas kernels, store(): pl.pallas_call(functools.partial(store_kernel, len(arrays), parts), out_s...  10.4 us

profile of v3, /device:TPU:0, one launch (start us, length us, event | category | flops | bytes accessed | tf_op | source)
XLA Modules:
  0.0 123.3 jit_solution(2602383635645186378)
XLA Ops:
  0.6 112.3 %shard_map.117 = (bf16[3072,2048]{1,0:T(8,128)(2,1)S(1)}, bf16[3072,2048]{1,0:T(8,128)(2,1)S(1)}, f32[1,2048]{1,0:T(1,128)S(1)}, f32[1,2048]{1,0:T(1,128)S(1)}, ...) custom-call(f32[384,2048]{1,0:T(8,128)} %weight_gate.1, f32[384,2048]{1,0:T(8,128)} %smooth_gate.1, ...), custom_call_target="tpu_custom_call" | custom-call | tf_op jit(solution)/shard_map/pallas_call | solution.py:399
  112.9 10.4 %shard_map.118 = (bf16[3072,2048]{1,0:T(8,128)(2,1)}, bf16[3072,2048]{1,0:T(8,128)(2,1)}, f32[1,2048]{1,0:T(1,128)}, f32[1,2048]{1,0:T(1,128)}, bf16[24,128]{1,0...) custom-call(bf16[3072,2048]{1,0:T(8,128)(2,1)S(1)} %get-tuple-element.21.refs_0_, ...), custom_call_target="tpu_custom_call" | custom-call | tf_op jit(solution)/shard_map/pallas_call | solution.py:373

commit v4 on v3

--- a/solution.py
+++ b/solution.py
@@ -21,30 +21,42 @@
     return chips // nx, nx
 
 
-def pieces_of(cols, early):
+def pieces_of(rows, cols, ends):
     tiles = cols // LANES
-    found = []
+    cut = rows * 3 // 4 // 16 * 16
+    found, tails = [], []
     for unit in range(2):
+        at = 0
         queues = []
         for along_x, many in ((True, (tiles + 1) // 2), (False, tiles // 2)):
-            if many < 3:
-                widths = [1] * many
+            if many < 4 or not ends:
+                queues.append([(along_x, 1, None)] * many)
+            elif unit == 0:
+                queues.append([(along_x, 2, None), (along_x, 1, "early"), (along_x, many - 3, None)])
             else:
-                widths = [1, 1, many - 2] if unit == 0 else [many - 1, 1]
-            queues.append((along_x, widths))
-        at = 0
-        for n in range(max(len(q) for _, q in queues)):
-            for along_x, widths in queues:
-                if n < len(widths):
-                    found.append((unit, at * LANES, widths[n] * LANES, along_x, early and unit == 0 and n == 1))
-                    at += widths[n]
+                queues.append([(along_x, many - 1, None), (along_x, 1, "last")])
+        for n in range(max(len(q) for q in queues)):
+            for queue in queues:
+                if n < len(queue):
+                    along_x, width, kind = queue[n]
+                    here = (unit, at * LANES, width * LANES)
+                    at += width
+                    if kind is None:
+                        found.append(here + (0, rows, along_x, None))
+                    else:
+                        found.append(here + (0, cut, along_x, "early" if kind == "early" else None))
+                        tails.append(here + (cut, rows - cut, along_x, "last" if kind == "last" else None))
+        found += tails
+        tails = []
     return found
 
 
 def spans_of(pieces):
     spans = []
-    for unit, at, width, _, _ in pieces:
-        if spans and spans[-1][0] == unit and spans[-1][2] + width <= 2 * LANES:
+    for unit, at, width, top, _, _, _ in pieces:
+        if top:
+            continue
+        if spans and spans[-1][0] == unit and spans[-1][2] == width and width <= 2 * LANES:
             spans[-1] = (unit, spans[-1][1], spans[-1][2] + width)
         else:
             spans.append((unit, at, width))
@@ -55,8 +67,8 @@
     n_shard, n_model, ny, nx, pieces, spans,
     weight_gate, smooth_gate, weight_up, smooth_up, norm_train, norm_step,
     serve_gate, serve_up, factor_gate, factor_up, norm_out, whole_gate, whole_up,
-    inputs, peaks, early, norm_in, norm_mine, norm_all, norm_rows,
-    load_sem, peak_recv, ring_recv, second_recv, pair_recv, sent_sem, small_sem,
+    inputs, peaks, chip_peaks, early, norm_in, norm_mine, norm_all, norm_rows,
+    load_sem, peak_send, peak_recv, couple_recv, ring_recv, second_recv, pair_recv, both_recv, sent_sem, small_sem,
 ):
     me = lax.axis_index("shard")
     col = lax.axis_index("model")
@@ -69,11 +81,13 @@
     rows, cols = whole_gate.shape
     serves, wholes, factors = (serve_gate, serve_up), (whole_gate, whole_up), (factor_gate, factor_up)
     order = range(len(pieces))
-    early_pieces = [p for p in order if pieces[p][4]]
+    early_pieces = [p for p in order if pieces[p][6] == "early"]
+    last_pieces = [p for p in order if pieces[p][6] == "last"]
+    chips = ny * nx
     lead = 1
     is_lead = me == lead
     per = norm_train.shape[1]
-    norm_load, peak_send, mine_send, mine_recv, z_send, z_recv, all_send, all_recv = [small_sem.at[i] for i in range(8)]
+    norm_load, mine_send, mine_recv, z_send, z_recv, all_send, all_recv = [small_sem.at[i] for i in range(7)]
 
     def across(p):
         return pl.ds(pieces[p][1], pieces[p][2])
@@ -81,11 +95,20 @@
     def wait_bytes(ref, sem):
         pltpu.make_async_copy(ref, ref, sem).wait()
 
+    def blob(halves):
+        wide = next(
+            w for w in range(LANES, cols + 1, LANES) if halves % (8 * w) == 0 and halves // w <= n_shard * rows
+        )
+        return serve_gate.at[pl.ds(0, halves // wide), pl.ds(0, wide)]
+
     groups = [[], [], []]
     for p in order:
-        groups[2 if pieces[p][0] else int(pieces[p][1] >= 2 * LANES)].append(p)
-    reach = [(pieces[g[0]][0], pieces[g[0]][1], sum(pieces[p][2] for p in g)) for g in groups if g]
+        unit, at = pieces[p][:2]
+        groups[2 if unit else int(at >= sum(spans[0][1:]))].append(p)
     groups = [g for g in groups if g]
+    reach = [
+        (pieces[g[0]][0], pieces[g[0]][1], sum(pieces[p][2] for p in g if pieces[p][3] == 0)) for g in groups
+    ]
 
     sources = ((weight_gate, smooth_gate), (weight_up, smooth_up))
     for n, (unit, at, width) in enumerate(spans):
@@ -125,21 +148,34 @@
             device_id=device, device_id_type=MESH,
         ).start()
 
+    def across_group(g):
+        return pl.ds(reach[g][1], reach[g][2])
+
     def send_peaks(g):
-        unit, at, width = reach[g]
-        ref = peaks.at[unit, me, :, pl.ds(at, width)]
-        for d in range(1, n_shard):
-            start(ref, ref, (lax.rem(me + d, n_shard), col), peak_send, peak_recv.at[g])
+        ref = peaks.at[reach[g][0], me, :, across_group(g)]
+        if g == 0:
+            for d in range(1, n_shard):
+                start(ref, ref, (lax.rem(me + d, n_shard), col), peak_send.at[g], peak_recv.at[g])
+        else:
+            start(ref, ref, (pair, col), peak_send.at[g], couple_recv.at[g])
+
+    def combine_peaks(g):
+        unit, here = reach[g][0], across_group(g)
+        wait_bytes(peaks.at[unit, 0, :, here], couple_recv.at[g])
+        chip_peaks[unit, chip, :, here] = jnp.maximum(peaks[unit, me, :, here], peaks[unit, pair, :, here])
+
+    def spread_peaks(g):
+        ref = chip_peaks.at[reach[g][0], chip, :, across_group(g)]
+        for d in range(1, chips):
+            start(ref, ref, (lax.rem(me + 2 * d, n_shard), col), peak_send.at[g], peak_recv.at[g])
 
     def piece_of(p, dy, dx, side):
         owner = (lax.rem(ypos - dy + ny, ny) * nx + lax.rem(xpos - dx + nx, nx)) * 2 + side
-        return serves[pieces[p][0]].at[pl.ds(pl.multiple_of(owner * rows, rows), rows), across(p)]
-
-    def group_of(p):
-        return 2 if pieces[p][4] else pieces[p][0]
+        unit, _, _, top, height = pieces[p][:5]
+        return serves[unit].at[pl.ds(pl.multiple_of(owner * rows + top, 16), height), across(p)]
 
     def along_x_first(p):
-        return pieces[p][3]
+        return pieces[p][5]
 
     def on_second_way(p, dy, dx):
         return (dy, dx) == ((1, 0) if along_x_first(p) else (0, 1))
@@ -152,19 +188,35 @@
             return second_recv.at[pieces[p][0]]
         return ring_recv.at[landings.index((p, dy, dx))]
 
+    sent = [0, 0, 0]
+    paired = [0, 0]
+
+    def send(p, spot, device, sem):
+        ref = piece_of(p, *spot, core)
+        kind = 2 if p in early_pieces else pieces[p][0]
+        sent[kind] += pieces[p][2] * pieces[p][4]
+        start(ref, ref, (device, col), sent_sem.at[kind], sem)
+
+    def both_cores(p, dy, dx):
+        return p in last_pieces and (dy, dx) == (ny - 1, nx - 1)
+
+    def onward(p, spot, device, there):
+        send(p, spot, device, landing(p, *there))
+        if both_cores(p, *there):
+            send(p, spot, device + 1 - 2 * core, both_recv.at[last_pieces.index(p)])
+
     def to_x(p, dy, dx):
         if dx < nx - 1 and (dy == 0 or not along_x_first(p)):
-            ref = piece_of(p, dy, dx, core)
-            start(ref, ref, (x_next, col), sent_sem.at[group_of(p)], landing(p, dy, dx + 1))
+            onward(p, (dy, dx), x_next, (dy, dx + 1))
 
     def to_y(p, dy, dx):
         if dy < ny - 1 and (dx == 0 or along_x_first(p)):
-            ref = piece_of(p, dy, dx, core)
-            start(ref, ref, (y_next, col), sent_sem.at[group_of(p)], landing(p, dy + 1, dx))
+            onward(p, (dy, dx), y_next, (dy + 1, dx))
 
     def to_pair(p, dy, dx):
-        ref = piece_of(p, dy, dx, core)
-        start(ref, ref, (pair, col), sent_sem.at[group_of(p)], pair_recv.at[pieces[p][0]])
+        if not both_cores(p, dy, dx):
+            paired[pieces[p][0]] += pieces[p][2] * pieces[p][4]
+            send(p, (dy, dx), pair, pair_recv.at[pieces[p][0]])
 
     def first_way(p):
         (to_x if along_x_first(p) else to_y)(p, 0, 0)
@@ -172,10 +224,11 @@
     def second_way(p):
         (to_y if along_x_first(p) else to_x)(p, 0, 0)
 
-    chunks = 4 if rows % 32 == 0 else 1
+    cut = pieces[early_pieces[0]][4] if early_pieces else 0
+    chunks = 3 if cut % 24 == 0 else 1
 
     def send_early(chunk):
-        span = pl.ds(chunk * (rows // chunks), rows // chunks)
+        span = pl.ds(chunk * (cut // chunks), cut // chunks)
         for n, p in enumerate(early_pieces):
             device, spot = (x_next, (0, 1)) if along_x_first(p) else (y_next, (1, 0))
             start(
@@ -184,27 +237,28 @@
             )
 
     def landed_early(p, dy, dx):
-        return pieces[p][4] and (dy, dx) == ((0, 1) if along_x_first(p) else (1, 0))
+        return p in early_pieces and (dy, dx) == ((0, 1) if along_x_first(p) else (1, 0))
 
     def find_factor(g):
-        unit, at, width = reach[g]
-        here = pl.ds(at, width)
-        wait_bytes(peaks.at[unit, pl.ds(0, n_shard - 1), :, here], peak_recv.at[g])
-        factor = peaks[unit, 0, :, here]
-        for d in range(1, n_shard):
-            factor = jnp.maximum(factor, peaks[unit, d, :, here])
+        unit, here = reach[g][0], across_group(g)
+        table, many = (peaks, n_shard) if g == 0 else (chip_peaks, chips)
+        if many > 1:
+            wait_bytes(table.at[unit, pl.ds(0, many - 1), :, here], peak_recv.at[g])
+        factor = table[unit, 0, :, here]
+        for d in range(1, many):
+            factor = jnp.maximum(factor, table[unit, d, :, here])
         factors[unit][:, here] = factor
 
     def narrow(p, owner, read):
-        unit = pieces[p][0]
+        unit, _, _, top, height = pieces[p][:5]
 
         def step(i, carry):
-            at = i * 16
+            at = top + i * 16
             value = read(pl.ds(pl.multiple_of(at, 16), 16)) / factors[unit][:, across(p)]
             serves[unit][pl.ds(pl.multiple_of(owner * rows + at, 16), 16), across(p)] = value.astype(jnp.bfloat16)
             return carry
 
-        lax.fori_loop(0, rows // 16, step, 0, unroll=2)
+        lax.fori_loop(0, height // 16, step, 0, unroll=2)
 
     def narrow_own(p):
         narrow(p, me, lambda span: wholes[pieces[p][0]][span, across(p)])
@@ -214,7 +268,7 @@
     def arrived(p, dy, dx):
         if landed_early(p, dy, dx):
             n = early_pieces.index(p)
-            wait_bytes(early.at[n], landing(p, dy, dx))
+            wait_bytes(early.at[n, pl.ds(0, cut)], landing(p, dy, dx))
             owner = (lax.rem(ypos - dy + ny, ny) * nx + lax.rem(xpos - dx + nx, nx)) * 2 + core
             narrow(p, owner, lambda span: early[n, span])
         elif not on_second_way(p, dy, dx):
@@ -254,20 +308,21 @@
     def _():
         pl.semaphore_wait(barrier, n_shard - 1)
 
-    ends = [at + width for _, at, width in reach]
     ready, chunk = 0, 0
     for n, (unit, at, width) in enumerate(spans):
+        final = n == len(spans) - 1
+        if final and ready > 1:
+            combine_peaks(1)
         if n:
             average(n)
-        if (unit, at + width) == (reach[ready][0], ends[ready]):
+        if (unit, at + width) == (reach[ready][0], sum(reach[ready][1:])):
             send_peaks(ready)
             ready += 1
-        if n and chunk < chunks:
+        if n and chunk < chunks and early_pieces:
             send_early(chunk)
             chunk += 1
-    while chunk < chunks:
-        send_early(chunk)
-        chunk += 1
+    if len(groups) > 1:
+        spread_peaks(1)
 
     for g, group in enumerate(groups):
         find_factor(g)
@@ -285,7 +340,11 @@
         if before is not None:
             first_way(before)
         if g == 0:
+            for later in range(2, len(groups)):
+                combine_peaks(later)
             norm_to_lead()
+            for later in range(2, len(groups)):
+                spread_peaks(later)
     norm_spread()
     for p in order:
         if p not in early_pieces:
@@ -332,24 +391,23 @@
             if distance == 1 and own_way:
                 gather_norm()
 
-    spread = len(early_pieces) * LANES
-    hops = 2 * ny * nx - 1
     for unit in range(2):
-        wait_bytes(serves[unit].at[pl.ds(0, ny * nx * rows)], pair_recv.at[unit])
-    wait_bytes(serve_gate.at[pl.ds(0, hops * rows), pl.ds(0, cols - spread)], sent_sem.at[0])
-    wait_bytes(serve_up.at[pl.ds(0, hops * rows)], sent_sem.at[1])
-    if early_pieces:
-        wait_bytes(serve_gate.at[pl.ds(0, (hops - 1) * rows), pl.ds(0, spread)], sent_sem.at[2])
+        wait_bytes(blob(paired[unit]), pair_recv.at[unit])
+    for n, p in enumerate(last_pieces):
+        wait_bytes(piece_of(p, ny - 1, nx - 1, 1 - core), both_recv.at[n])
+    for kind, halves in enumerate(sent):
+        if halves:
+            wait_bytes(blob(halves), sent_sem.at[kind])
     for n in range(len(early_pieces)):
-        wait_bytes(early.at[n], sent_sem.at[3 + n])
-    wait_bytes(peaks.at[:, pl.ds(0, n_shard - 1)], peak_send)
+        wait_bytes(early.at[n, pl.ds(0, cut)], sent_sem.at[3 + n])
+    wait_bytes(peaks.at[0, pl.ds(0, n_shard - 1), :, across_group(0)], peak_send.at[0])
+    for g in range(1, len(groups)):
+        wait_bytes(chip_peaks.at[reach[g][0], :, :, across_group(g)], peak_send.at[g])
 
     @pl.when(is_lead)
     def _():
         wait_bytes(norm_all.at[pl.ds(0, n_model - 1)], z_send)
-        halves = (n_shard - 1) * math.prod(norm_all.shape) * 2
-        wide = next(w for w in (LANES << k for k in range(16)) if halves // w <= n_shard * rows)
-        wait_bytes(serve_gate.at[pl.ds(0, halves // wide), pl.ds(0, wide)], all_send)
+        wait_bytes(blob((n_shard - 1) * math.prod(norm_all.shape) * 2), all_send)
 
     @pl.when(jnp.logical_not(is_lead))
     def _():
@@ -387,7 +445,7 @@
     def body(weight_gate, smooth_gate, weight_up, smooth_up, norm_train, norm_step):
         rows, cols = weight_gate.shape
         per = norm_train.shape[0]
-        pieces = pieces_of(cols, min(nx, ny) > 1)
+        pieces = pieces_of(rows, cols, min(nx, ny) > 1)
         spans = spans_of(pieces)
         count = len(pieces)
         wide = -(-per // LANES) * LANES
@@ -412,6 +470,7 @@
             scratch_shapes=[
                 pltpu.VMEM((2, 2, rows, cols), jnp.float32),
                 pltpu.VMEM((2, n_shard, 1, cols), jnp.float32),
+                pltpu.VMEM((2, ny * nx, 1, cols), jnp.float32),
                 pltpu.VMEM((2, rows, LANES), jnp.float32),
                 pltpu.VMEM((2, 1, per), jnp.float32),
                 pltpu.VMEM((1, wide), jnp.float32),
@@ -419,11 +478,14 @@
                 pltpu.VMEM((tiles, LANES), jnp.float32),
                 dma((len(spans),)),
                 dma((3,)),
+                dma((3,)),
+                dma((3,)),
                 dma((count * (ny * nx - 2),)),
                 dma((2,)),
                 dma((2,)),
+                dma((2,)),
                 dma((5,)),
-                dma((8,)),
+                dma((7,)),
             ],
             compiler_params=pltpu.CompilerParams(
                 collective_id=0, has_side_effects=True, vmem_limit_bytes=20 * 1024 * 1024

time: 123 us -> 122 us (level)
  no operation moved by 1% of the time
where the time goes in v4:
time: 122 us
  Pallas kernels  122 us (100%)
    pallas_call x1, Pallas kernels, body(): pl.pallas_call(functools.partial(kernel, n_shard, n_model, ny, nx, pieces...  111 us
    pallas_call x1, Pallas kernels, store(): pl.pallas_call(functools.partial(store_kernel, len(arrays), parts), out_s...  10.4 us

profile of v4, /device:TPU:0, one launch (start us, length us, event | category | flops | bytes accessed | tf_op | source)
XLA Modules:
  0.0 122.3 jit_solution(12108552266642043558)
XLA Ops:
  0.6 111.3 %shard_map.117 = (bf16[3072,2048]{1,0:T(8,128)(2,1)S(1)}, bf16[3072,2048]{1,0:T(8,128)(2,1)S(1)}, f32[1,2048]{1,0:T(1,128)S(1)}, f32[1,2048]{1,0:T(1,128)S(1)}, ...) custom-call(f32[384,2048]{1,0:T(8,128)} %weight_gate.1, f32[384,2048]{1,0:T(8,128)} %smooth_gate.1, ...), custom_call_target="tpu_custom_call" | custom-call | tf_op jit(solution)/shard_map/pallas_call | solution.py:457
  111.9 10.4 %shard_map.118 = (bf16[3072,2048]{1,0:T(8,128)(2,1)}, bf16[3072,2048]{1,0:T(8,128)(2,1)}, f32[1,2048]{1,0:T(1,128)}, f32[1,2048]{1,0:T(1,128)}, bf16[24,128]{1,0...) custom-call(bf16[3072,2048]{1,0:T(8,128)(2,1)S(1)} %get-tuple-element.21.refs_0_, ...), custom_call_target="tpu_custom_call" | custom-call | tf_op jit(solution)/shard_map/pallas_call | solution.py:431

commit v5 on v4

--- a/solution.py
+++ b/solution.py
@@ -34,15 +34,16 @@
             elif unit == 0:
                 queues.append([(along_x, 2, None), (along_x, 1, "early"), (along_x, many - 3, None)])
             else:
-                queues.append([(along_x, many - 1, None), (along_x, 1, "last")])
+                near = many // 2
+                queues.append([(along_x, near, "near"), (along_x, many - near - 1, None), (along_x, 1, "last")])
         for n in range(max(len(q) for q in queues)):
             for queue in queues:
                 if n < len(queue):
                     along_x, width, kind = queue[n]
                     here = (unit, at * LANES, width * LANES)
                     at += width
-                    if kind is None:
-                        found.append(here + (0, rows, along_x, None))
+                    if kind in (None, "near"):
+                        found.append(here + (0, rows, along_x, kind))
                     else:
                         found.append(here + (0, cut, along_x, "early" if kind == "early" else None))
                         tails.append(here + (cut, rows - cut, along_x, "last" if kind == "last" else None))
@@ -66,7 +67,7 @@
 def kernel(
     n_shard, n_model, ny, nx, pieces, spans,
     weight_gate, smooth_gate, weight_up, smooth_up, norm_train, norm_step,
-    serve_gate, serve_up, factor_gate, factor_up, norm_out, whole_gate, whole_up,
+    serve_gate, serve_up, factor_gate, factor_up, norm_out, whole_gate, whole_up, block,
     inputs, peaks, chip_peaks, early, norm_in, norm_mine, norm_all, norm_rows,
     load_sem, peak_send, peak_recv, couple_recv, ring_recv, second_recv, pair_recv, both_recv, sent_sem, small_sem,
 ):
@@ -83,6 +84,8 @@
     order = range(len(pieces))
     early_pieces = [p for p in order if pieces[p][6] == "early"]
     last_pieces = [p for p in order if pieces[p][6] == "last"]
+    near_pieces = [p for p in order if pieces[p][6] == "near"]
+    far = (ny - 1, nx - 1)
     chips = ny * nx
     lead = 1
     is_lead = me == lead
@@ -182,6 +185,7 @@
 
     landings = [(p, dy, dx) for p in order for dy in range(ny) for dx in range(nx)]
     landings = [spot for spot in landings if spot[1:] != (0, 0) and not on_second_way(*spot)]
+    landings = [spot for spot in landings if not (spot[0] in near_pieces and spot[1:] == far)]
 
     def landing(p, dy, dx):
         if on_second_way(p, dy, dx):
@@ -189,7 +193,7 @@
         return ring_recv.at[landings.index((p, dy, dx))]
 
     sent = [0, 0, 0]
-    paired = [0, 0]
+    paired = [0, 0, 0]
 
     def send(p, spot, device, sem):
         ref = piece_of(p, *spot, core)
@@ -198,9 +202,11 @@
         start(ref, ref, (device, col), sent_sem.at[kind], sem)
 
     def both_cores(p, dy, dx):
-        return p in last_pieces and (dy, dx) == (ny - 1, nx - 1)
+        return p in last_pieces and (dy, dx) == far
 
     def onward(p, spot, device, there):
+        if p in near_pieces and there == far:
+            return
         send(p, spot, device, landing(p, *there))
         if both_cores(p, *there):
             send(p, spot, device + 1 - 2 * core, both_recv.at[last_pieces.index(p)])
@@ -215,8 +221,9 @@
 
     def to_pair(p, dy, dx):
         if not both_cores(p, dy, dx):
-            paired[pieces[p][0]] += pieces[p][2] * pieces[p][4]
-            send(p, (dy, dx), pair, pair_recv.at[pieces[p][0]])
+            kind = 2 if p in near_pieces else pieces[p][0]
+            paired[kind] += pieces[p][2] * pieces[p][4]
+            send(p, (dy, dx), pair, pair_recv.at[kind])
 
     def first_way(p):
         (to_x if along_x_first(p) else to_y)(p, 0, 0)
@@ -377,17 +384,39 @@
             norm_rows[t:t + 1] = tile[0:1]
         norm_out[...] = norm_rows[...].astype(jnp.bfloat16)
 
+    def fill_block():
+        wait_bytes(blob(paired[2]), pair_recv.at[2])
+        chosen = lax.rem(ypos + 1 + core, ny) * nx + lax.rem(xpos + 2 - core, nx)
+        base = 2 * rows * chosen
+        width = block.shape[1]
+        for c in range(2):
+            @pl.when(core == c)
+            def _():
+                def step(i, carry):
+                    block[pl.ds(pl.multiple_of(i * 16, 16), 16)] = serve_up[
+                        pl.ds(pl.multiple_of(base + i * 16, 16), 16), c * width:(c + 1) * width
+                    ]
+                    return carry
+
+                lax.fori_loop(0, 2 * rows // 16, step, 0, unroll=4)
+
+    block_due = bool(near_pieces)
     for distance in range(1, ny + nx - 1):
         for own_way in (True, False):
             for p in order:
                 for dy in range(ny):
                     dx = distance - dy
                     straight = (dy if along_x_first(p) else dx) == 0
+                    if p in near_pieces and (dy, dx) == far:
+                        continue
                     if 0 <= dx < nx and straight == own_way:
                         arrived(p, dy, dx)
                         to_x(p, dy, dx)
                         to_y(p, dy, dx)
                         to_pair(p, dy, dx)
+                        if block_due and (dy, dx) == far:
+                            block_due = False
+                            fill_block()
             if distance == 1 and own_way:
                 gather_norm()
 
@@ -435,17 +464,54 @@
         out_specs=(hbm,) * len(arrays),
         scratch_shapes=[pltpu.SemaphoreType.DMA((len(arrays),))],
         compiler_params=pltpu.CompilerParams(vmem_limit_bytes=1024 * 1024),
+        cost_estimate=pl.CostEstimate(flops=10**9, bytes_accessed=0, transcendentals=0),
     )(*(pltpu.with_memory_space_constraint(a, pltpu.VMEM) for a in arrays))
+
+
+def patch_kernel(ny, nx, serve, direct, swapped, out, sem):
+    me = lax.axis_index("shard")
+    core = lax.rem(me, 2)
+    chip = me // 2
+    missing = lax.rem(chip // nx + 1, ny) * nx + lax.rem(lax.rem(chip, nx) + 1, nx)
+    height, width = direct.shape
+    span = pl.ds(pl.multiple_of(missing * height, height), height)
+    for n, (src, side) in enumerate(((direct, core), (swapped, 1 - core))):
+        dst = out.at[span, pl.ds(pl.multiple_of(side * width, width), width)]
+        pltpu.make_async_copy(src, dst, sem.at[n]).start()
+    for n, src in enumerate((direct, swapped)):
+        pltpu.make_async_copy(src, out.at[span, pl.ds(0, width)], sem.at[n]).wait()
+
+
+def patch(ny, nx, serve, direct, swapped):
+    hbm = pl.BlockSpec(memory_space=pltpu.HBM)
+    vmem = pl.BlockSpec(memory_space=pltpu.VMEM)
+    return pl.pallas_call(
+        functools.partial(patch_kernel, ny, nx),
+        out_shape=pltpu.HBM(serve.shape, serve.dtype),
+        in_specs=[hbm, vmem, vmem],
+        out_specs=hbm,
+        scratch_shapes=[pltpu.SemaphoreType.DMA((2,))],
+        input_output_aliases={0: 0},
+        compiler_params=pltpu.CompilerParams(vmem_limit_bytes=1024 * 1024),
+    )(serve, *(pltpu.with_memory_space_constraint(a, pltpu.VMEM) for a in (direct, swapped)))
 
 
 def solution(mesh):
     n_shard, n_model = mesh.shape["shard"], mesh.shape["model"]
     ny, nx = grid_of(n_shard)
+    onward_pairs, swap_pairs = [], []
+    for chip in range(ny * nx):
+        y, x = divmod(chip, nx)
+        beside, above = y * nx + (x + 1) % nx, (y + 1) % ny * nx + x
+        onward_pairs += [(2 * chip, 2 * beside), (2 * chip + 1, 2 * above + 1)]
+        swap_pairs += [(2 * chip, 2 * chip + 1), (2 * chip + 1, 2 * chip)]
 
     def body(weight_gate, smooth_gate, weight_up, smooth_up, norm_train, norm_step):
         rows, cols = weight_gate.shape
         per = norm_train.shape[0]
-        pieces = pieces_of(rows, cols, min(nx, ny) > 1)
+        ends = min(nx, ny) > 1 and cols % (8 * LANES) == 0
+        pieces = pieces_of(rows, cols, ends)
+        reach = cols // LANES // 4 * LANES if ends else LANES
         spans = spans_of(pieces)
         count = len(pieces)
         wide = -(-per // LANES) * LANES
@@ -464,9 +530,10 @@
                 pltpu.VMEM((tiles, LANES), jnp.bfloat16),
                 pltpu.VMEM((rows, cols), jnp.float32),
                 pltpu.VMEM((rows, cols), jnp.float32),
+                pltpu.VMEM((2 * rows, reach), jnp.bfloat16),
             ),
             in_specs=[hbm] * 6,
-            out_specs=(vmem,) * 7,
+            out_specs=(vmem,) * 8,
             scratch_shapes=[
                 pltpu.VMEM((2, 2, rows, cols), jnp.float32),
                 pltpu.VMEM((2, n_shard, 1, cols), jnp.float32),
@@ -482,7 +549,7 @@
                 dma((3,)),
                 dma((count * (ny * nx - 2),)),
                 dma((2,)),
-                dma((2,)),
+                dma((3,)),
                 dma((2,)),
                 dma((5,)),
                 dma((7,)),
@@ -496,7 +563,16 @@
                 for a in (weight_gate, smooth_gate, weight_up, smooth_up, norm_train[None], norm_step[None])
             ),
         )
-        serve_gate, serve_up, factor_gate, factor_up, norm, whole_gate, whole_up = store(landed, 4)
+        *landed, whole_up, block = landed
+        if ends:
+            direct = lax.ppermute(block, "shard", onward_pairs)
+        serve_gate, serve_up, factor_gate, factor_up, norm, whole_gate = store(landed, 4)
+        if ends:
+            direct, whole_up, serve_up = lax.optimization_barrier((direct, whole_up, serve_up))
+            swapped = lax.ppermute(direct, "shard", swap_pairs)
+        (whole_up,) = store([whole_up], 4)
+        if ends:
+            serve_up = patch(ny, nx, serve_up, direct, swapped)
         return (
             serve_gate, serve_up, factor_gate.reshape(-1), factor_up.reshape(-1),
             norm.reshape(-1)[:width], whole_gate, whole_up,

time: 122 us -> 119 us (0.975)
  Pallas kernels: 122 us -> 115 us
  starting transfers between devices: 0 us -> 2.27 us
    pallas_call x1, Pallas kernels: 111 us -> 102 us  [body(): pl.pallas_call(functools.partial(kernel, n_shard, n_model, ny, nx, pieces...]
    ppermute x0 -> x2, starting transfers between devices: none -> 2.27 us  [the longest x1 2.27 us: body(): direct = lax.ppermute(block, 'shard', onward_pairs)]
    pallas_call x1 -> x2, Pallas kernels: 10.4 us -> 11.1 us  [store(): pl.pallas_call(functools.partial(store_kernel, len(arrays), parts), out_s...]
  transfers between devices with their start and end apart: 0 -> 2, of which waited for: 0 -> 2; matrix products, arithmetic and copies ran while one was open for 0% -> 0% of each run, Pallas kernels for 0% -> 9%
where the time goes in v5:
time: 119 us
  Pallas kernels  115 us (97%)
  starting transfers between devices  2.27 us (2%)
    pallas_call x1, Pallas kernels, body(): pl.pallas_call(functools.partial(kernel, n_shard, n_model, ny, nx, pieces...  102 us
    pallas_call x2, Pallas kernels, store(): pl.pallas_call(functools.partial(store_kernel, len(arrays), parts), out_s...  11.1 us
  transfers between devices with their start and end apart: 2, of which 2 were waited for; matrix products, arithmetic and copies ran while one was open for 0% of the time, Pallas kernels for 9%

profile of v5, /device:TPU:0, one launch (start us, length us, event | category | flops | bytes accessed | tf_op | source)
XLA Modules:
  0.0 118.7 jit_solution(14316130235223407546)
XLA Ops:
  0.6 102.4 %shard_map.117 = (bf16[3072,2048]{1,0:T(8,128)(2,1)S(1)}, bf16[3072,2048]{1,0:T(8,128)(2,1)S(1)}, f32[1,2048]{1,0:T(1,128)S(1)}, f32[1,2048]{1,0:T(1,128)S(1)}, ...) custom-call(f32[384,2048]{1,0:T(8,128)} %weight_gate.1, ...), custom_call_target="tpu_custom_call" | custom-call | tf_op jit(solution)/shard_map/pallas_call | solution.py:523
  103.0 2.3 %collective-permute-start = (bf16[768,512]{1,0:T(8,128)(2,1)S(1)}, bf16[768,512]{1,0:T(8,128)(2,1)S(1)}, u32[]{:S(2)}, u32[]{:S(2)}) collective-permute-start(bf16[768,512]{1,0:T(8,128)(2,1)S(1)} %get-tuple-element.31), channel_id=1, source_target_pairs={{0,8},{4,20},{8,0},{12,28},{16,24},{20,4},{24,16},{28,12},{1,9},{5... | collective-permute-start | bytes 2359304 | tf_op jit(solution)/shard_map/ppermute | solution.py:568
  105.3 9.4 %shard_map.118 = (bf16[3072,2048]{1,0:T(8,128)(2,1)}, bf16[3072,2048]{1,0:T(8,128)(2,1)}, f32[1,2048]{1,0:T(1,128)}, f32[1,2048]{1,0:T(1,128)}, bf16[24,128]{1,0:T(8,128)(2,1)}, /*index=5*/f32[384,2048]{1,0:T(8,128)}) custom-call(bf16[3072,2048]{1,0:T(8,128)(2,1)S(1)} %get-tuple-element.24.refs_0_, bf16[3072,2048]{1,0:T(8,128)(2,1)S(1)} %get-tuple-element.25.refs_1_, ...), custom_call_target="tpu_custom_call" | custom-call | flops 1000000000 | tf_op jit(solution)/shard_map/pallas_call | solution.py:460
  114.7 0.6 collective-permute-done.direct
  115.2 0.0 collective-permute-start.1
  115.2 1.7 %shard_map.120 = f32[384,2048]{1,0:T(8,128)} custom-call(f32[384,2048]{1,0:T(8,128)S(1)} %get-tuple-element.40.refs_0_), custom_call_target="tpu_custom_call" | custom-call | flops 1000000000 | tf_op jit(solution)/shard_map/pallas_call | solution.py:460
  116.9 0.6 collective-permute-done.1.swapped
  117.5 1.2 shard_map.119
Async XLA Ops:
  103.0 12.2 %collective-permute-start = (bf16[768,512]{1,0:T(8,128)(2,1)S(1)}, bf16[768,512]{1,0:T(8,128)(2,1)S(1)}, u32[]{:S(2)}, u32[]{:S(2)}) collective-permute-start(bf16[768,512]{1,0:T(8,128)(2,1)S(1)} %get-tuple-element.31), channel_id=1, source_target_pairs={{0,8},{4,20},{8,0},{12,28},{16,24},{20,4},{24,16},{28,12},{1,9},{5... | collective-permute-start | bytes 2359304 | tf_op jit(solution)/shard_map/ppermute | solution.py:568
  115.2 2.3 %collective-permute-start.1 = (bf16[768,512]{1,0:T(8,128)(2,1)S(1)}, bf16[768,512]{1,0:T(8,128)(2,1)S(1)}, u32[]{:S(2)}, u32[]{:S(2)}) collective-permute-start(bf16[768,512]{1,0:T(8,128)(2,1)S(1)} %collective-permute-done.direct), channel_id=1, source_target_pairs={{0,4},{4,0},{8,12},{12,8},{16,20},{20,16},{24,28},{28,24},{1,5},{5... | collective-permute-start | bytes 2359304 | tf_op jit(solution)/shard_map/ppermute | solution.py:572

commit v6 on v5

--- a/solution.py
+++ b/solution.py
@@ -35,20 +35,42 @@
                 queues.append([(along_x, 2, None), (along_x, 1, "early"), (along_x, many - 3, None)])
             else:
                 near = many // 2
-                queues.append([(along_x, near, "near"), (along_x, many - near - 1, None), (along_x, 1, "last")])
+                queues.append([(along_x, near, "near"), (along_x, many - near - 1, None), (along_x, 1, "loose")])
         for n in range(max(len(q) for q in queues)):
             for queue in queues:
                 if n < len(queue):
                     along_x, width, kind = queue[n]
                     here = (unit, at * LANES, width * LANES)
                     at += width
-                    if kind in (None, "near"):
+                    if kind == "early":
+                        found.append(here + (0, cut, along_x, kind))
+                        tails.append(here + (cut, rows - cut, along_x, None))
+                    else:
                         found.append(here + (0, rows, along_x, kind))
-                    else:
-                        found.append(here + (0, cut, along_x, "early" if kind == "early" else None))
-                        tails.append(here + (cut, rows - cut, along_x, "last" if kind == "last" else None))
         found += tails
         tails = []
+    return found
+
+
+def is_early_landing(piece, dy, dx):
+    return piece[6] == "early" and (dy, dx) == ((0, 1) if piece[5] else (1, 0))
+
+
+def landings_of(pieces, ny, nx):
+    found = {}
+    far = (ny - 1, nx - 1)
+    for p, piece in enumerate(pieces):
+        unit, along_x, kind = piece[0], piece[5], piece[6]
+        for dy in range(ny):
+            for dx in range(nx):
+                if (dy, dx) == (0, 0) or (kind == "near" and (dy, dx) == far):
+                    continue
+                key = (unit, along_x, dy, dx)
+                if (dy, dx) == ((1, 0) if along_x else (0, 1)):
+                    key = unit
+                elif is_early_landing(piece, dy, dx) or (unit and (dy, dx) == far):
+                    key = (p, dy, dx)
+                found.setdefault(key, []).append((p, dy, dx))
     return found
 
 
@@ -67,9 +89,9 @@
 def kernel(
     n_shard, n_model, ny, nx, pieces, spans,
     weight_gate, smooth_gate, weight_up, smooth_up, norm_train, norm_step,
-    serve_gate, serve_up, factor_gate, factor_up, norm_out, whole_gate, whole_up, block,
+    serve_gate, serve_up, factor_gate, factor_up, norm_out, whole_gate, whole_up, block, loose,
     inputs, peaks, chip_peaks, early, norm_in, norm_mine, norm_all, norm_rows,
-    load_sem, peak_send, peak_recv, couple_recv, ring_recv, second_recv, pair_recv, both_recv, sent_sem, small_sem,
+    load_sem, peak_send, peak_recv, couple_recv, ring_recv, pair_recv, sent_sem, small_sem,
 ):
     me = lax.axis_index("shard")
     col = lax.axis_index("model")
@@ -83,7 +105,7 @@
     serves, wholes, factors = (serve_gate, serve_up), (whole_gate, whole_up), (factor_gate, factor_up)
     order = range(len(pieces))
     early_pieces = [p for p in order if pieces[p][6] == "early"]
-    last_pieces = [p for p in order if pieces[p][6] == "last"]
+    loose_pieces = [p for p in order if pieces[p][6] == "loose"]
     near_pieces = [p for p in order if pieces[p][6] == "near"]
     far = (ny - 1, nx - 1)
     chips = ny * nx
@@ -113,6 +135,15 @@
         (pieces[g[0]][0], pieces[g[0]][1], sum(pieces[p][2] for p in g if pieces[p][3] == 0)) for g in groups
     ]
 
+    barrier = pltpu.get_barrier_semaphore()
+    for d in range(1, n_shard):
+        pl.semaphore_signal(barrier, inc=1, device_id=(lax.rem(me + d, n_shard), col), device_id_type=MESH)
+
+    @pl.when(is_lead)
+    def _():
+        for d in range(1, n_model):
+            pl.semaphore_signal(barrier, inc=1, device_id=(me, lax.rem(col + d, n_model)), device_id_type=MESH)
+
     sources = ((weight_gate, smooth_gate), (weight_up, smooth_up))
     for n, (unit, at, width) in enumerate(spans):
         for which in range(2):
@@ -122,15 +153,6 @@
     for i, src in enumerate((norm_train, norm_step)):
         pltpu.make_async_copy(src, norm_in.at[i], norm_load).start()
 
-    barrier = pltpu.get_barrier_semaphore()
-    for d in range(1, n_shard):
-        pl.semaphore_signal(barrier, inc=1, device_id=(lax.rem(me + d, n_shard), col), device_id_type=MESH)
-
-    @pl.when(is_lead)
-    def _():
-        for d in range(1, n_model):
-            pl.semaphore_signal(barrier, inc=1, device_id=(me, lax.rem(col + d, n_model)), device_id_type=MESH)
-
     def average(n):
         unit, first, width = spans[n]
         here = pl.ds(first, width)
@@ -180,36 +202,34 @@
     def along_x_first(p):
         return pieces[p][5]
 
-    def on_second_way(p, dy, dx):
-        return (dy, dx) == ((1, 0) if along_x_first(p) else (0, 1))
-
-    landings = [(p, dy, dx) for p in order for dy in range(ny) for dx in range(nx)]
-    landings = [spot for spot in landings if spot[1:] != (0, 0) and not on_second_way(*spot)]
-    landings = [spot for spot in landings if not (spot[0] in near_pieces and spot[1:] == far)]
+    def landed_early(p, dy, dx):
+        return is_early_landing(pieces[p], dy, dx)
+
+    gathers = landings_of(pieces, ny, nx)
+    keys = list(gathers)
+
+    def key_of(p, dy, dx):
+        return next(key for key in keys if (p, dy, dx) in gathers[key])
 
     def landing(p, dy, dx):
-        if on_second_way(p, dy, dx):
-            return second_recv.at[pieces[p][0]]
-        return ring_recv.at[landings.index((p, dy, dx))]
+        return ring_recv.at[keys.index(key_of(p, dy, dx))]
 
     sent = [0, 0, 0]
     paired = [0, 0, 0]
 
-    def send(p, spot, device, sem):
+    def send(p, spot, device, sem, dst=None):
         ref = piece_of(p, *spot, core)
         kind = 2 if p in early_pieces else pieces[p][0]
         sent[kind] += pieces[p][2] * pieces[p][4]
-        start(ref, ref, (device, col), sent_sem.at[kind], sem)
-
-    def both_cores(p, dy, dx):
-        return p in last_pieces and (dy, dx) == far
+        start(ref, ref if dst is None else dst, (device, col), sent_sem.at[kind], sem)
+
+    def loose_ref(p):
+        return loose.at[:, pl.ds(loose_pieces.index(p) * LANES, LANES)]
 
     def onward(p, spot, device, there):
         if p in near_pieces and there == far:
             return
-        send(p, spot, device, landing(p, *there))
-        if both_cores(p, *there):
-            send(p, spot, device + 1 - 2 * core, both_recv.at[last_pieces.index(p)])
+        send(p, spot, device, landing(p, *there), loose_ref(p) if p in loose_pieces and there == far else None)
 
     def to_x(p, dy, dx):
         if dx < nx - 1 and (dy == 0 or not along_x_first(p)):
@@ -220,7 +240,7 @@
             onward(p, (dy, dx), y_next, (dy + 1, dx))
 
     def to_pair(p, dy, dx):
-        if not both_cores(p, dy, dx):
+        if not (p in loose_pieces and (dy, dx) == far):
             kind = 2 if p in near_pieces else pieces[p][0]
             paired[kind] += pieces[p][2] * pieces[p][4]
             send(p, (dy, dx), pair, pair_recv.at[kind])
@@ -242,9 +262,6 @@
                 wholes[pieces[p][0]].at[span, across(p)], early.at[n, span], (device, col),
                 sent_sem.at[3 + n], landing(p, *spot),
             )
-
-    def landed_early(p, dy, dx):
-        return p in early_pieces and (dy, dx) == ((0, 1) if along_x_first(p) else (1, 0))
 
     def find_factor(g):
         unit, here = reach[g][0], across_group(g)
@@ -270,19 +287,20 @@
     def narrow_own(p):
         narrow(p, me, lambda span: wholes[pieces[p][0]][span, across(p)])
 
-    seconds = set()
+    here_now = set()
 
     def arrived(p, dy, dx):
+        key = key_of(p, dy, dx)
+        if key not in here_now:
+            here_now.add(key)
+            if landed_early(p, dy, dx):
+                wait_bytes(early.at[early_pieces.index(p), pl.ds(0, cut)], landing(p, dy, dx))
+            else:
+                wait_bytes(blob(sum(pieces[q][2] * pieces[q][4] for q, _, _ in gathers[key])), landing(p, dy, dx))
         if landed_early(p, dy, dx):
             n = early_pieces.index(p)
-            wait_bytes(early.at[n, pl.ds(0, cut)], landing(p, dy, dx))
             owner = (lax.rem(ypos - dy + ny, ny) * nx + lax.rem(xpos - dx + nx, nx)) * 2 + core
             narrow(p, owner, lambda span: early[n, span])
-        elif not on_second_way(p, dy, dx):
-            wait_bytes(piece_of(p, dy, dx, core), landing(p, dy, dx))
-        elif pieces[p][0] not in seconds:
-            seconds.add(pieces[p][0])
-            wait_bytes(serves[pieces[p][0]].at[pl.ds(0, rows)], landing(p, dy, dx))
 
     def norm_sum():
         wait_bytes(norm_in, norm_load)
@@ -422,8 +440,6 @@
 
     for unit in range(2):
         wait_bytes(blob(paired[unit]), pair_recv.at[unit])
-    for n, p in enumerate(last_pieces):
-        wait_bytes(piece_of(p, ny - 1, nx - 1, 1 - core), both_recv.at[n])
     for kind, halves in enumerate(sent):
         if halves:
             wait_bytes(blob(halves), sent_sem.at[kind])
@@ -468,32 +484,47 @@
     )(*(pltpu.with_memory_space_constraint(a, pltpu.VMEM) for a in arrays))
 
 
-def patch_kernel(ny, nx, serve, direct, swapped, out, sem):
+def patch_kernel(ny, nx, kinds, *refs):
     me = lax.axis_index("shard")
     core = lax.rem(me, 2)
     chip = me // 2
     missing = lax.rem(chip // nx + 1, ny) * nx + lax.rem(lax.rem(chip, nx) + 1, nx)
-    height, width = direct.shape
-    span = pl.ds(pl.multiple_of(missing * height, height), height)
-    for n, (src, side) in enumerate(((direct, core), (swapped, 1 - core))):
-        dst = out.at[span, pl.ds(pl.multiple_of(side * width, width), width)]
-        pltpu.make_async_copy(src, dst, sem.at[n]).start()
-    for n, src in enumerate((direct, swapped)):
-        pltpu.make_async_copy(src, out.at[span, pl.ds(0, width)], sem.at[n]).wait()
-
-
-def patch(ny, nx, serve, direct, swapped):
+    blocks, rest, sem = refs[1:1 + len(kinds)], refs[1 + len(kinds):-1], refs[-1]
+    extra, (out, *stored) = rest[:len(rest) // 2], rest[len(rest) // 2:]
+    waits = []
+    for n, (kind, src) in enumerate(zip(kinds, blocks)):
+        height, width = src.shape
+        if kind in ("direct", "swapped"):
+            row = missing * height
+            side = core if kind == "direct" else 1 - core
+            across = pl.ds(pl.multiple_of(side * width, width), width)
+        else:
+            row = (2 * missing + (core if kind == "loose" else 1 - core)) * height
+            across = pl.ds(out.shape[1] - width, width)
+        span = pl.ds(pl.multiple_of(row, 16), height)
+        waits.append(pltpu.make_async_copy(src, out.at[span, across], sem.at[n]))
+        waits[-1].start()
+    for n, (src, dst) in enumerate(zip(extra, stored)):
+        waits.append(pltpu.make_async_copy(src, dst, sem.at[len(kinds) + n]))
+        waits[-1].start()
+    for copy in waits:
+        copy.wait()
+
+
+def patch(ny, nx, serve, blocks, extra=()):
     hbm = pl.BlockSpec(memory_space=pltpu.HBM)
     vmem = pl.BlockSpec(memory_space=pltpu.VMEM)
+    held = (*blocks.values(), *extra)
     return pl.pallas_call(
-        functools.partial(patch_kernel, ny, nx),
-        out_shape=pltpu.HBM(serve.shape, serve.dtype),
-        in_specs=[hbm, vmem, vmem],
-        out_specs=hbm,
-        scratch_shapes=[pltpu.SemaphoreType.DMA((2,))],
+        functools.partial(patch_kernel, ny, nx, tuple(blocks)),
+        out_shape=tuple(pltpu.HBM(a.shape, a.dtype) for a in (serve, *extra)),
+        in_specs=[hbm] + [vmem] * len(held),
+        out_specs=(hbm,) * (1 + len(extra)),
+        scratch_shapes=[pltpu.SemaphoreType.DMA((len(held),))],
         input_output_aliases={0: 0},
         compiler_params=pltpu.CompilerParams(vmem_limit_bytes=1024 * 1024),
-    )(serve, *(pltpu.with_memory_space_constraint(a, pltpu.VMEM) for a in (direct, swapped)))
+        cost_estimate=pl.CostEstimate(flops=10**9, bytes_accessed=0, transcendentals=0),
+    )(serve, *(pltpu.with_memory_space_constraint(a, pltpu.VMEM) for a in held))
 
 
 def solution(mesh):
@@ -531,9 +562,10 @@
                 pltpu.VMEM((rows, cols), jnp.float32),
                 pltpu.VMEM((rows, cols), jnp.float32),
                 pltpu.VMEM((2 * rows, reach), jnp.bfloat16),
+                pltpu.VMEM((rows, 2 * LANES), jnp.bfloat16),
             ),
             in_specs=[hbm] * 6,
-            out_specs=(vmem,) * 8,
+            out_specs=(vmem,) * 9,
             scratch_shapes=[
                 pltpu.VMEM((2, 2, rows, cols), jnp.float32),
                 pltpu.VMEM((2, n_shard, 1, cols), jnp.float32),
@@ -547,10 +579,8 @@
                 dma((3,)),
                 dma((3,)),
                 dma((3,)),
-                dma((count * (ny * nx - 2),)),
-                dma((2,)),
+                dma((len(landings_of(pieces, ny, nx)),)),
                 dma((3,)),
-                dma((2,)),
                 dma((5,)),
                 dma((7,)),
             ],
@@ -563,16 +593,21 @@
                 for a in (weight_gate, smooth_gate, weight_up, smooth_up, norm_train[None], norm_step[None])
             ),
         )
-        *landed, whole_up, block = landed
+        *landed, whole_up, block, loose = landed
         if ends:
             direct = lax.ppermute(block, "shard", onward_pairs)
+            paired = lax.ppermute(loose, "shard", swap_pairs)
         serve_gate, serve_up, factor_gate, factor_up, norm, whole_gate = store(landed, 4)
         if ends:
-            direct, whole_up, serve_up = lax.optimization_barrier((direct, whole_up, serve_up))
+            direct, paired, loose, whole_up, serve_up = lax.optimization_barrier(
+                (direct, paired, loose, whole_up, serve_up)
+            )
             swapped = lax.ppermute(direct, "shard", swap_pairs)
-        (whole_up,) = store([whole_up], 4)
-        if ends:
-            serve_up = patch(ny, nx, serve_up, direct, swapped)
+            first = {"direct": direct, "loose": loose, "paired": paired}
+            serve_up, whole_up = patch(ny, nx, serve_up, first, (whole_up,))
+            (serve_up,) = patch(ny, nx, serve_up, {"swapped": swapped})
+        else:
+            (whole_up,) = store([whole_up], 4)
         return (
             serve_gate, serve_up, factor_gate.reshape(-1), factor_up.reshape(-1),
             norm.reshape(-1)[:width], whole_gate, whole_up,

time: 119 us -> 117 us (0.983)
    pallas_call x1 -> x2, Pallas kernels: 1.15 us -> 2.97 us  [patch(): pl.pallas_call(functools.partial(patch_kernel, ny, nx, tuple(blocks)), ou...]
    pallas_call x2 -> x1, Pallas kernels: 11.1 us -> 9.4 us  [store(): pl.pallas_call(functools.partial(store_kernel, len(arrays), parts), out_s...]
  transfers between devices with their start and end apart: 2 -> 3, of which waited for: 2 -> 2; matrix products, arithmetic and copies ran while one was open for 0% -> 0% of each run, Pallas kernels for 9% -> 10%
where the time goes in v6:
time: 117 us
  Pallas kernels  114 us (97%)
  starting transfers between devices  2.24 us (2%)
    pallas_call x1, Pallas kernels, body(): pl.pallas_call(functools.partial(kernel, n_shard, n_model, ny, nx, pieces...  101 us
    pallas_call x1, Pallas kernels, store(): pl.pallas_call(functools.partial(store_kernel, len(arrays), parts), out_s...  9.4 us
    pallas_call x2, Pallas kernels, patch(): pl.pallas_call(functools.partial(patch_kernel, ny, nx, tuple(blocks)), ou...  2.97 us
  transfers between devices with their start and end apart: 3, of which 2 were waited for; matrix products, arithmetic and copies ran while one was open for 0% of the time, Pallas kernels for 10%

profile of v6, /device:TPU:0, one launch (start us, length us, event | category | flops | bytes accessed | tf_op | source)
XLA Modules:
  0.0 117.3 jit_solution(10004607899543709435)
XLA Ops:
  0.6 101.3 %shard_map.117 = (bf16[3072,2048]{1,0:T(8,128)(2,1)S(1)}, bf16[3072,2048]{1,0:T(8,128)(2,1)S(1)}, f32[1,2048]{1,0:T(1,128)S(1)}, f32[1,2048]{1,0:T(1,128)S(1)}, ...) custom-call(f32[384,2048]{1,0:T(8,128)} %weight_gate.1, ...), custom_call_target="tpu_custom_call" | custom-call | tf_op jit(solution)/shard_map/pallas_call | solution.py:554
  102.0 2.2 %collective-permute-start = (bf16[768,512]{1,0:T(8,128)(2,1)S(1)}, bf16[768,512]{1,0:T(8,128)(2,1)S(1)}, u32[]{:S(2)}, u32[]{:S(2)}) collective-permute-start(bf16[768,512]{1,0:T(8,128)(2,1)S(1)} %get-tuple-element.36), channel_id=1, source_target_pairs={{0,8},{4,20},{8,0},{12,28},{16,24},{20,4},{24,16},{28,12},{1,9},{5... | collective-permute-start | bytes 2359304 | tf_op jit(solution)/shard_map/ppermute | solution.py:598
  104.2 0.0 collective-permute-start.1
  104.2 9.4 %shard_map.118 = (bf16[3072,2048]{1,0:T(8,128)(2,1)}, bf16[3072,2048]{1,0:T(8,128)(2,1)}, f32[1,2048]{1,0:T(1,128)}, f32[1,2048]{1,0:T(1,128)}, bf16[24,128]{1,0:T(8,128)(2,1)}, /*index=5*/f32[384,2048]{1,0:T(8,128)}) custom-call(bf16[3072,2048]{1,0:T(8,128)(2,1)S(1)} %get-tuple-element.29.refs_0_, bf16[3072,2048]{1,0:T(8,128)(2,1)S(1)} %get-tuple-element.30.refs_1_, ...), custom_call_target="tpu_custom_call" | custom-call | flops 1000000000 | tf_op jit(solution)/shard_map/pallas_call | solution.py:476
  113.6 0.0 collective-permute-done.1.refs_3_
  113.6 0.6 collective-permute-done.refs_1_
  114.2 0.0 collective-permute-start.2
  114.2 2.1 %shard_map.119 = (bf16[3072,2048]{1,0:T(8,128)(2,1)}, f32[384,2048]{1,0:T(8,128)}) custom-call(bf16[3072,2048]{1,0:T(8,128)(2,1)} %get-tuple-element.40.refs_0_, bf16[768,512]{1,0:T(8,128)(2,1)S(1)} %collective-permute-done.refs_1_, bf16[384,256]{1,0:T(8,128)(2,1)S(1)} %get-tuple-element.42.refs_2_, ...), custom_call_target="tpu_custom_call", output_to_operand_aliasing={{0}: (0, {})} | custom-call | flops 1000000000 | tf_op jit(solution)/shard_map/pallas_call | solution.py:518
  116.3 0.2 collective-permute-done.2.refs_1_
  116.4 0.9 shard_map.120
Async XLA Ops:
  102.0 12.2 %collective-permute-start = (bf16[768,512]{1,0:T(8,128)(2,1)S(1)}, bf16[768,512]{1,0:T(8,128)(2,1)S(1)}, u32[]{:S(2)}, u32[]{:S(2)}) collective-permute-start(bf16[768,512]{1,0:T(8,128)(2,1)S(1)} %get-tuple-element.36), channel_id=1, source_target_pairs={{0,8},{4,20},{8,0},{12,28},{16,24},{20,4},{24,16},{28,12},{1,9},{5... | collective-permute-start | bytes 2359304 | tf_op jit(solution)/shard_map/ppermute | solution.py:598
  104.2 9.4 %collective-permute-start.1 = (bf16[384,256]{1,0:T(8,128)(2,1)S(1)}, bf16[384,256]{1,0:T(8,128)(2,1)S(1)}, u32[]{:S(2)}, u32[]{:S(2)}) collective-permute-start(bf16[384,256]{1,0:T(8,128)(2,1)S(1)} %get-tuple-element.42.refs_2_), channel_id=1, source_target_pairs={{0,4},{4,0},{8,12},{12,8},{16,20},{20,16},{24,28},{28,24},{1,5},{5... | collective-permute-start | bytes 589832 | tf_op jit(solution)/shard_map/ppermute | solution.py:599
  114.2 2.3 %collective-permute-start.2 = (bf16[768,512]{1,0:T(8,128)(2,1)S(1)}, bf16[768,512]{1,0:T(8,128)(2,1)S(1)}, u32[]{:S(2)}, u32[]{:S(2)}) collective-permute-start(bf16[768,512]{1,0:T(8,128)(2,1)S(1)} %collective-permute-done.refs_1_), channel_id=1, source_target_pairs={{0,4},{4,0},{8,12},{12,8},{16,20},{20,16},{24,28},{28,24},{1,5},{5... | collective-permute-start | bytes 2359304 | tf_op jit(solution)/shard_map/ppermute | solution.py:605

commit v7 on v6

--- a/solution.py
+++ b/solution.py
@@ -302,6 +302,24 @@
             owner = (lax.rem(ypos - dy + ny, ny) * nx + lax.rem(xpos - dx + nx, nx)) * 2 + core
             narrow(p, owner, lambda span: early[n, span])
 
+    def gather_norm():
+        lane = lax.broadcasted_iota(jnp.int32, (8, LANES), 1)
+        tiles = [jnp.zeros((8, LANES), jnp.float32) for _ in range(norm_out.shape[0])]
+        for s in range(n_shard):
+            for c in range(n_model):
+                for at in range(0, per, LANES):
+                    size = min(LANES, per - at)
+                    tile, shift = divmod((s * n_model + c) * per + at, LANES)
+                    row = jnp.broadcast_to(norm_all[c, s, :, at:at + LANES], (8, LANES))
+                    if shift:
+                        row = pltpu.roll(row, shift, 1)
+                    tiles[tile] = jnp.where((lane >= shift) & (lane < shift + size), row, tiles[tile])
+                    if shift + size > LANES:
+                        tiles[tile + 1] = jnp.where(lane < shift + size - LANES, row, tiles[tile + 1])
+        for t, tile in enumerate(tiles):
+            norm_rows[t:t + 1] = tile[0:1]
+        norm_out[...] = norm_rows[...].astype(jnp.bfloat16)
+
     def norm_sum():
         wait_bytes(norm_in, norm_load)
         norm_mine[...] = jnp.zeros(norm_mine.shape, jnp.float32)
@@ -320,8 +338,20 @@
             for d in range(1, n_model):
                 start(norm_all.at[col], norm_all.at[col], (me, lax.rem(col + d, n_model)), z_send, z_recv)
             wait_bytes(norm_all.at[pl.ds(0, n_model - 1)], z_recv)
-            for d in range(1, n_shard):
-                start(norm_all, norm_all, (lax.rem(me + d, n_shard), col), all_send, all_recv)
+            gather_norm()
+
+    def norm_out_to_chips():
+        @pl.when(is_lead)
+        def _():
+            for d in range(1, chips):
+                start(norm_out, norm_out, (lax.rem(me + 2 * d, n_shard), col), all_send, all_recv)
+            start(norm_out, norm_out, (pair, col), all_send, all_recv)
+
+    def norm_out_to_pair():
+        @pl.when(jnp.logical_and(core == 1, jnp.logical_not(is_lead)))
+        def _():
+            wait_bytes(norm_out, all_recv)
+            start(norm_out, norm_out, (pair, col), all_send, all_recv)
 
     average(0)
 
@@ -371,36 +401,15 @@
             for later in range(2, len(groups)):
                 spread_peaks(later)
     norm_spread()
+    for group in groups[1:]:
+        for p in group:
+            to_pair(p, 0, 0)
+    norm_out_to_chips()
     for p in order:
         if p not in early_pieces:
             second_way(p)
     for p in early_pieces:
         second_way(p)
-    for group in groups[1:]:
-        for p in group:
-            to_pair(p, 0, 0)
-
-    def gather_norm():
-        @pl.when(jnp.logical_not(is_lead))
-        def _():
-            wait_bytes(norm_all, all_recv)
-
-        lane = lax.broadcasted_iota(jnp.int32, (8, LANES), 1)
-        tiles = [jnp.zeros((8, LANES), jnp.float32) for _ in range(norm_out.shape[0])]
-        for s in range(n_shard):
-            for c in range(n_model):
-                for at in range(0, per, LANES):
-                    size = min(LANES, per - at)
-                    tile, shift = divmod((s * n_model + c) * per + at, LANES)
-                    row = jnp.broadcast_to(norm_all[c, s, :, at:at + LANES], (8, LANES))
-                    if shift:
-                        row = pltpu.roll(row, shift, 1)
-                    tiles[tile] = jnp.where((lane >= shift) & (lane < shift + size), row, tiles[tile])
-                    if shift + size > LANES:
-                        tiles[tile + 1] = jnp.where(lane < shift + size - LANES, row, tiles[tile + 1])
-        for t, tile in enumerate(tiles):
-            norm_rows[t:t + 1] = tile[0:1]
-        norm_out[...] = norm_rows[...].astype(jnp.bfloat16)
 
     def fill_block():
         wait_bytes(blob(paired[2]), pair_recv.at[2])
@@ -436,7 +445,7 @@
                             block_due = False
                             fill_block()
             if distance == 1 and own_way:
-                gather_norm()
+                norm_out_to_pair()
 
     for unit in range(2):
         wait_bytes(blob(paired[unit]), pair_recv.at[unit])
@@ -452,11 +461,19 @@
     @pl.when(is_lead)
     def _():
         wait_bytes(norm_all.at[pl.ds(0, n_model - 1)], z_send)
-        wait_bytes(blob((n_shard - 1) * math.prod(norm_all.shape) * 2), all_send)
+        wait_bytes(blob(chips * math.prod(norm_out.shape)), all_send)
 
     @pl.when(jnp.logical_not(is_lead))
     def _():
         wait_bytes(norm_mine, mine_send)
+
+    @pl.when(jnp.logical_and(core == 1, jnp.logical_not(is_lead)))
+    def _():
+        wait_bytes(norm_out, all_send)
+
+    @pl.when(core == 0)
+    def _():
+        wait_bytes(norm_out, all_recv)
 
 
 def store_kernel(count, parts, *refs):

time: 117 us -> 117 us (level)
  no operation moved by 1% of the time
where the time goes in v7:
time: 117 us
  Pallas kernels  114 us (97%)
  starting transfers between devices  1.85 us (2%)
    pallas_call x1, Pallas kernels, body(): pl.pallas_call(functools.partial(kernel, n_shard, n_model, ny, nx, pieces...  101 us
    pallas_call x1, Pallas kernels, store(): pl.pallas_call(functools.partial(store_kernel, len(arrays), parts), out_s...  9.4 us
    pallas_call x2, Pallas kernels, patch(): pl.pallas_call(functools.partial(patch_kernel, ny, nx, tuple(blocks)), ou...  2.97 us
  transfers between devices with their start and end apart: 3, of which 2 were waited for; matrix products, arithmetic and copies ran while one was open for 0% of the time, Pallas kernels for 10%

profile of v7, /device:TPU:0, one launch (start us, length us, event | category | flops | bytes accessed | tf_op | source)
XLA Modules:
  0.0 117.2 jit_solution(16913399923814003899)
XLA Ops:
  0.6 101.3 %shard_map.117 = (bf16[3072,2048]{1,0:T(8,128)(2,1)S(1)}, bf16[3072,2048]{1,0:T(8,128)(2,1)S(1)}, f32[1,2048]{1,0:T(1,128)S(1)}, f32[1,2048]{1,0:T(1,128)S(1)}, ...) custom-call(f32[384,2048]{1,0:T(8,128)} %weight_gate.1, ...), custom_call_target="tpu_custom_call" | custom-call | tf_op jit(solution)/shard_map/pallas_call | solution.py:571
  102.0 1.8 %collective-permute-start = (bf16[768,512]{1,0:T(8,128)(2,1)S(1)}, bf16[768,512]{1,0:T(8,128)(2,1)S(1)}, u32[]{:S(2)}, u32[]{:S(2)}) collective-permute-start(bf16[768,512]{1,0:T(8,128)(2,1)S(1)} %get-tuple-element.36), channel_id=1, source_target_pairs={{0,8},{4,20},{8,0},{12,28},{16,24},{20,4},{24,16},{28,12},{1,9},{5... | collective-permute-start | bytes 2359304 | tf_op jit(solution)/shard_map/ppermute | solution.py:615
  103.8 0.0 collective-permute-start.1
  103.8 9.4 %shard_map.118 = (bf16[3072,2048]{1,0:T(8,128)(2,1)}, bf16[3072,2048]{1,0:T(8,128)(2,1)}, f32[1,2048]{1,0:T(1,128)}, f32[1,2048]{1,0:T(1,128)}, bf16[24,128]{1,0:T(8,128)(2,1)}, /*index=5*/f32[384,2048]{1,0:T(8,128)}) custom-call(bf16[3072,2048]{1,0:T(8,128)(2,1)S(1)} %get-tuple-element.29.refs_0_, bf16[3072,2048]{1,0:T(8,128)(2,1)S(1)} %get-tuple-element.30.refs_1_, ...), custom_call_target="tpu_custom_call" | custom-call | flops 1000000000 | tf_op jit(solution)/shard_map/pallas_call | solution.py:493
  113.2 0.0 collective-permute-done.1.refs_3_
  113.2 0.8 collective-permute-done.refs_1_
  114.0 0.0 collective-permute-start.2
  114.0 2.1 %shard_map.119 = (bf16[3072,2048]{1,0:T(8,128)(2,1)}, f32[384,2048]{1,0:T(8,128)}) custom-call(bf16[3072,2048]{1,0:T(8,128)(2,1)} %get-tuple-element.40.refs_0_, bf16[768,512]{1,0:T(8,128)(2,1)S(1)} %collective-permute-done.refs_1_, bf16[384,256]{1,0:T(8,128)(2,1)S(1)} %get-tuple-element.42.refs_2_, ...), custom_call_target="tpu_custom_call", output_to_operand_aliasing={{0}: (0, {})} | custom-call | flops 1000000000 | tf_op jit(solution)/shard_map/pallas_call | solution.py:535
  116.1 0.2 collective-permute-done.2.refs_1_
  116.3 0.9 shard_map.120
Async XLA Ops:
  102.0 12.1 %collective-permute-start = (bf16[768,512]{1,0:T(8,128)(2,1)S(1)}, bf16[768,512]{1,0:T(8,128)(2,1)S(1)}, u32[]{:S(2)}, u32[]{:S(2)}) collective-permute-start(bf16[768,512]{1,0:T(8,128)(2,1)S(1)} %get-tuple-element.36), channel_id=1, source_target_pairs={{0,8},{4,20},{8,0},{12,28},{16,24},{20,4},{24,16},{28,12},{1,9},{5... | collective-permute-start | bytes 2359304 | tf_op jit(solution)/shard_map/ppermute | solution.py:615
  103.8 9.4 %collective-permute-start.1 = (bf16[384,256]{1,0:T(8,128)(2,1)S(1)}, bf16[384,256]{1,0:T(8,128)(2,1)S(1)}, u32[]{:S(2)}, u32[]{:S(2)}) collective-permute-start(bf16[384,256]{1,0:T(8,128)(2,1)S(1)} %get-tuple-element.42.refs_2_), channel_id=1, source_target_pairs={{0,4},{4,0},{8,12},{12,8},{16,20},{20,16},{24,28},{28,24},{1,5},{5... | collective-permute-start | bytes 589832 | tf_op jit(solution)/shard_map/ppermute | solution.py:616
  114.0 2.3 %collective-permute-start.2 = (bf16[768,512]{1,0:T(8,128)(2,1)S(1)}, bf16[768,512]{1,0:T(8,128)(2,1)S(1)}, u32[]{:S(2)}, u32[]{:S(2)}) collective-permute-start(bf16[768,512]{1,0:T(8,128)(2,1)S(1)} %collective-permute-done.refs_1_), channel_id=1, source_target_pairs={{0,4},{4,0},{8,12},{12,8},{16,20},{20,16},{24,28},{28,24},{1,5},{5... | collective-permute-start | bytes 2359304 | tf_op jit(solution)/shard_map/ppermute | solution.py:622

commit v8 on v7

--- a/solution.py
+++ b/solution.py
@@ -483,7 +483,7 @@
         size = src.shape[0] // pieces
         for part in range(pieces):
             span = pl.ds(part * size, size)
-            pltpu.make_async_copy(src.at[span], dst.at[span], refs[-1].at[n]).start()
+            pltpu.make_async_copy(src.at[span], dst.at[span], refs[-1].at[n]).start(priority=(part + n) % 2)
     for n, (src, dst) in enumerate(pairs):
         pltpu.make_async_copy(src, dst, refs[-1].at[n]).wait()
 
@@ -614,7 +614,7 @@
         if ends:
             direct = lax.ppermute(block, "shard", onward_pairs)
             paired = lax.ppermute(loose, "shard", swap_pairs)
-        serve_gate, serve_up, factor_gate, factor_up, norm, whole_gate = store(landed, 4)
+        serve_gate, serve_up, factor_gate, factor_up, norm, whole_gate = store(landed, 8)
         if ends:
             direct, paired, loose, whole_up, serve_up = lax.optimization_barrier(
                 (direct, paired, loose, whole_up, serve_up)

time: 117 us -> 117 us (level)
  no operation moved by 1% of the time
where the time goes in v8:
time: 117 us
  Pallas kernels  114 us (97%)
  starting transfers between devices  1.85 us (2%)
    pallas_call x1, Pallas kernels, body(): pl.pallas_call(functools.partial(kernel, n_shard, n_model, ny, nx, pieces...  101 us
    pallas_call x1, Pallas kernels, store(): pl.pallas_call(functools.partial(store_kernel, len(arrays), parts), out_s...  9.33 us
    pallas_call x2, Pallas kernels, patch(): pl.pallas_call(functools.partial(patch_kernel, ny, nx, tuple(blocks)), ou...  2.97 us
  transfers between devices with their start and end apart: 3, of which 2 were waited for; matrix products, arithmetic and copies ran while one was open for 0% of the time, Pallas kernels for 10%

profile of v8, /device:TPU:0, one launch (start us, length us, event | category | flops | bytes accessed | tf_op | source)
XLA Modules:
  0.0 117.2 jit_solution(15359766362841642385)
XLA Ops:
  0.6 101.3 %shard_map.117 = (bf16[3072,2048]{1,0:T(8,128)(2,1)S(1)}, bf16[3072,2048]{1,0:T(8,128)(2,1)S(1)}, f32[1,2048]{1,0:T(1,128)S(1)}, f32[1,2048]{1,0:T(1,128)S(1)}, ...) custom-call(f32[384,2048]{1,0:T(8,128)} %weight_gate.1, ...), custom_call_target="tpu_custom_call" | custom-call | tf_op jit(solution)/shard_map/pallas_call | solution.py:571
  102.0 1.8 %collective-permute-start = (bf16[768,512]{1,0:T(8,128)(2,1)S(1)}, bf16[768,512]{1,0:T(8,128)(2,1)S(1)}, u32[]{:S(2)}, u32[]{:S(2)}) collective-permute-start(bf16[768,512]{1,0:T(8,128)(2,1)S(1)} %get-tuple-element.36), channel_id=1, source_target_pairs={{0,8},{4,20},{8,0},{12,28},{16,24},{20,4},{24,16},{28,12},{1,9},{5... | collective-permute-start | bytes 2359304 | tf_op jit(solution)/shard_map/ppermute | solution.py:615
  103.8 0.0 collective-permute-start.1
  103.8 9.3 %shard_map.118 = (bf16[3072,2048]{1,0:T(8,128)(2,1)}, bf16[3072,2048]{1,0:T(8,128)(2,1)}, f32[1,2048]{1,0:T(1,128)}, f32[1,2048]{1,0:T(1,128)}, bf16[24,128]{1,0:T(8,128)(2,1)}, /*index=5*/f32[384,2048]{1,0:T(8,128)}) custom-call(bf16[3072,2048]{1,0:T(8,128)(2,1)S(1)} %get-tuple-element.29.refs_0_, bf16[3072,2048]{1,0:T(8,128)(2,1)S(1)} %get-tuple-element.30.refs_1_, ...), custom_call_target="tpu_custom_call" | custom-call | flops 1000000000 | tf_op jit(solution)/shard_map/pallas_call | solution.py:493
  113.2 0.0 collective-permute-done.1.refs_3_
  113.2 0.9 collective-permute-done.refs_1_
  114.0 0.0 collective-permute-start.2
  114.0 2.1 %shard_map.119 = (bf16[3072,2048]{1,0:T(8,128)(2,1)}, f32[384,2048]{1,0:T(8,128)}) custom-call(bf16[3072,2048]{1,0:T(8,128)(2,1)} %get-tuple-element.40.refs_0_, bf16[768,512]{1,0:T(8,128)(2,1)S(1)} %collective-permute-done.refs_1_, bf16[384,256]{1,0:T(8,128)(2,1)S(1)} %get-tuple-element.42.refs_2_, ...), custom_call_target="tpu_custom_call", output_to_operand_aliasing={{0}: (0, {})} | custom-call | flops 1000000000 | tf_op jit(solution)/shard_map/pallas_call | solution.py:535
  116.1 0.2 collective-permute-done.2.refs_1_
  116.3 0.9 shard_map.120
Async XLA Ops:
  102.0 12.1 %collective-permute-start = (bf16[768,512]{1,0:T(8,128)(2,1)S(1)}, bf16[768,512]{1,0:T(8,128)(2,1)S(1)}, u32[]{:S(2)}, u32[]{:S(2)}) collective-permute-start(bf16[768,512]{1,0:T(8,128)(2,1)S(1)} %get-tuple-element.36), channel_id=1, source_target_pairs={{0,8},{4,20},{8,0},{12,28},{16,24},{20,4},{24,16},{28,12},{1,9},{5... | collective-permute-start | bytes 2359304 | tf_op jit(solution)/shard_map/ppermute | solution.py:615
  103.8 9.3 %collective-permute-start.1 = (bf16[384,256]{1,0:T(8,128)(2,1)S(1)}, bf16[384,256]{1,0:T(8,128)(2,1)S(1)}, u32[]{:S(2)}, u32[]{:S(2)}) collective-permute-start(bf16[384,256]{1,0:T(8,128)(2,1)S(1)} %get-tuple-element.42.refs_2_), channel_id=1, source_target_pairs={{0,4},{4,0},{8,12},{12,8},{16,20},{20,16},{24,28},{28,24},{1,5},{5... | collective-permute-start | bytes 589832 | tf_op jit(solution)/shard_map/ppermute | solution.py:616
  114.0 2.3 %collective-permute-start.2 = (bf16[768,512]{1,0:T(8,128)(2,1)S(1)}, bf16[768,512]{1,0:T(8,128)(2,1)S(1)}, u32[]{:S(2)}, u32[]{:S(2)}) collective-permute-start(bf16[768,512]{1,0:T(8,128)(2,1)S(1)} %collective-permute-done.refs_1_), channel_id=1, source_target_pairs={{0,4},{4,0},{8,12},{12,8},{16,20},{20,16},{24,28},{28,24},{1,5},{5... | collective-permute-start | bytes 2359304 | tf_op jit(solution)/shard_map/ppermute | solution.py:622
